TPU v7x, 32 devices: a whole 2x2x4 slice. The times are simulated.
32 devices in a mesh: leaf: 16 (over z, y, core), top: 2 (over x).
Axes of the slice: x: 2, y: 2, z: 4, core: 2. Of those that a mesh axis runs over, the one named last changes fastest.
Arguments:
- vectors: bfloat16 [2, 16, 768, 512], P('top', 'leaf'), may hold values from -6 to 6
- near_tiles: bfloat16 [2, 16, 8, 768, 768], P('top', 'leaf'), may hold values from -0.078125 to 0.078125
- leaf_basis: bfloat16 [2, 16, 768, 128], P('top', 'leaf'), may hold values from -0.21875 to 0.21875
- transfer: bfloat16 [2, 16, 128, 128], P('top', 'leaf'), may hold values from -0.25 to 0.25
- coupling: bfloat16 [2, 16, 7, 128, 128], P('top', 'leaf'), may hold values from -0.1875 to 0.1875
- top_coupling: bfloat16 [2, 2, 128, 128], P('top'), may hold values from -0.375 to 0.375
- near_list: int32 [2, 16, 8], P('top', 'leaf'), may hold values from -4 to 4, as said below
- far_list: int32 [2, 16, 7], P('top', 'leaf'), may hold values from 0 to 15, as said below
- row_counts: int32 [2, 16], P('top', 'leaf'), may hold values from 384 to 768
Outputs:
- product: float32 [2, 16, 768, 512], P('top', 'leaf')
Inputs may be any that keep to these rules, and one draw needn't show every extreme that they name: `near_list`: each leaf's 8 offsets are distinct; an offset that leads outside the cluster's 16 leaves stands for an absent block. `far_list`: each leaf's entries are distinct positions in its cluster, each more than 4 away from the leaf's own position. `row_counts`: rows at and beyond the count are padding.
All inputs are finite; a program needn't handle non-finite values.
Results may differ from a plain program's by a relative error of at most 0.0045.
Values may be sent and summed in bfloat16 or wider, within the bound.
A program may use at most 128 MiB of HBM per device.

v0:
```python
import functools

import jax
import jax.numpy as jnp
from jax import lax
from jax.experimental import pallas as pl
from jax.experimental.pallas import tpu as pltpu
from jax.sharding import PartitionSpec as P

REACH = 4


def mirrored(index, bits):
    total = 0
    for bit in range(bits):
        total = total + lax.rem(lax.div(index, 1 << bit), 2) * (1 << (bits - 1 - bit))
    return total


def kernel(
    leaves,
    clusters,
    masked_ref,
    packed_ref,
    window,
    gathered,
    parents,
    send_sem,
    recv_sem,
    step_send,
    step_recv,
    top_send,
    top_recv,
    own_sem,
    same_sem,
):
    me = lax.axis_index("leaf")
    cluster = lax.axis_index("top")
    core = lax.rem(me, 2)
    toward = 1 - 2 * core
    partner = me + toward
    bits = leaves.bit_length() - 1
    vecs = masked_ref.shape[1]
    rank = packed_ref.shape[0]
    spot = mirrored(me, bits)

    own = pltpu.make_async_copy(
        packed_ref, gathered.at[pl.ds(pl.multiple_of(spot * rank, rank), rank)], own_sem
    )
    own.start()
    same = pltpu.make_async_copy(masked_ref, window.at[REACH], same_sem)
    same.start()

    def inside(offset):
        return jnp.logical_and(me + offset >= 0, me + offset < leaves)

    def peer_of(step):
        stride = leaves >> (step + 1)
        return me + stride * (1 - 2 * lax.rem(lax.div(me, stride), 2))

    barrier = pltpu.get_barrier_semaphore()
    expected = bits + clusters - 1
    for offset in (2, -2, 4, -4):
        expected = expected + inside(offset).astype(jnp.int32)

        @pl.when(inside(offset))
        def _(offset=offset):
            pl.semaphore_signal(
                barrier, inc=1, device_id={"leaf": me + offset}, device_id_type=pl.DeviceIdType.MESH
            )

    for step in range(bits):
        pl.semaphore_signal(
            barrier, inc=1, device_id={"leaf": peer_of(step)}, device_id_type=pl.DeviceIdType.MESH
        )
    for shift in range(1, clusters):
        pl.semaphore_signal(
            barrier,
            inc=1,
            device_id={"top": lax.rem(cluster + shift, clusters)},
            device_id_type=pl.DeviceIdType.MESH,
        )
    pl.semaphore_wait(barrier, expected)

    def exchange(step):
        size = 1 << step
        start = lax.div(spot, size) * size
        block = gathered.at[pl.ds(pl.multiple_of(start * rank, rank), size * rank)]
        return pltpu.make_async_remote_copy(
            src_ref=block,
            dst_ref=block,
            send_sem=step_send.at[step],
            recv_sem=step_recv.at[step],
            device_id={"leaf": peer_of(step)},
            device_id_type=pl.DeviceIdType.MESH,
        )

    def direct(offset):
        return pltpu.make_async_remote_copy(
            src_ref=masked_ref,
            dst_ref=window.at[REACH - offset],
            send_sem=send_sem.at[REACH + offset],
            recv_sem=recv_sem.at[REACH - offset],
            device_id={"leaf": me + offset},
            device_id_type=pl.DeviceIdType.MESH,
        )

    def forward(offset, slot):
        return pltpu.make_async_remote_copy(
            src_ref=masked_ref if offset == 0 else window.at[REACH + offset],
            dst_ref=window.at[REACH + offset - toward],
            send_sem=send_sem.at[slot],
            recv_sem=recv_sem.at[REACH + offset - toward],
            device_id={"leaf": partner},
            device_id_type=pl.DeviceIdType.MESH,
        )

    def forwarded(offset):
        if offset == 4:
            return jnp.logical_and(inside(offset), core == 0)
        if offset == -4:
            return jnp.logical_and(inside(offset), core == 1)
        return inside(offset)

    slot_of = {0: 1, 2: 3, -2: 5, 4: 7, -4: 4}

    def arrival(offset):
        block = window.at[REACH + offset]
        return pltpu.make_async_remote_copy(
            src_ref=block,
            dst_ref=block,
            send_sem=send_sem.at[REACH + offset],
            recv_sem=recv_sem.at[REACH + offset],
            device_id={"leaf": partner},
            device_id_type=pl.DeviceIdType.MESH,
        )

    own.wait()
    exchange(0).start()
    forward(0, slot_of[0]).start()
    for offset in (2, -2):

        @pl.when(inside(offset))
        def _(offset=offset):
            direct(offset).start()

    exchange(0).wait_recv()
    exchange(1).start()
    for offset in (4, -4):

        @pl.when(inside(offset))
        def _(offset=offset):
            direct(offset).start()

    exchange(1).wait_recv()
    exchange(2).start()
    for offset in (2, -2):

        @pl.when(inside(offset))
        def _(offset=offset):
            direct(-offset).wait_recv()
            forward(offset, slot_of[offset]).start()

    for step in range(2, bits):
        exchange(step).wait_recv()
        if step + 1 < bits:
            exchange(step + 1).start()

    def contract(left, right):
        return lax.dot_general(
            left, right, (((0,), (0,)), ((), ())), preferred_element_type=jnp.float32
        )

    parent = contract(gathered[:, vecs:], gathered[:, :vecs]).astype(jnp.bfloat16)
    parents[cluster] = parent

    for offset in (4, -4):

        @pl.when(inside(offset))
        def _(offset=offset):
            direct(-offset).wait_recv()

        @pl.when(forwarded(offset))
        def _(offset=offset):
            forward(offset, slot_of[offset]).start()

    def share(shift):
        return pltpu.make_async_remote_copy(
            src_ref=parents.at[cluster],
            dst_ref=parents.at[cluster],
            send_sem=top_send.at[shift],
            recv_sem=top_recv.at[shift],
            device_id={"top": lax.rem(cluster + shift, clusters)},
            device_id_type=pl.DeviceIdType.MESH,
        )

    for shift in range(1, clusters):
        share(shift).start()

    for offset in (1, -1, 3, -3):

        @pl.when(inside(offset))
        def _(offset=offset):
            arrival(offset).wait_recv()

    for shift in range(1, clusters):
        share(shift).wait_recv()
    same.wait()
    for step in range(bits):
        exchange(step).wait_send()
    for shift in range(1, clusters):
        share(shift).wait_send()
    for offset in (2, -2, 4, -4):

        @pl.when(inside(offset))
        def _(offset=offset):
            direct(offset).wait_send()

    for offset in (0, 2, -2, 4, -4):

        @pl.when(forwarded(offset))
        def _(offset=offset):
            forward(offset, slot_of[offset]).wait_send()


def local_kernel(
    clusters,
    slots,
    valid,
    places,
    scalars,
    tile_ref,
    source_ref,
    gathered,
    parents,
    basis_ref,
    nested_ref,
    coupling_ref,
    top_ref,
    out_ref,
):
    k = pl.program_id(0)
    rows, vecs = out_ref.shape
    rank = nested_ref.shape[0]
    part = rows // 3 if rows % 3 == 0 else rows

    @pl.when(k == 0)
    def _():
        out_ref[...] = jnp.zeros_like(out_ref)

    @pl.when(valid[k] == 1)
    def _():
        def piece(index, carry):
            span = pl.ds(pl.multiple_of(index * part, part), part)
            out_ref[span, :] += jnp.dot(
                tile_ref[0, span, :], source_ref[0], preferred_element_type=jnp.float32
            )
            return carry

        lax.fori_loop(0, rows // part, piece, 0)

    @pl.when(k == pl.num_programs(0) - 1)
    def _():
        field = jnp.zeros((rank, vecs), jnp.float32)
        for m in range(coupling_ref.shape[0]):
            start = pl.multiple_of(places[m] * rank, rank)
            field = field + jnp.dot(
                coupling_ref[m],
                gathered[pl.ds(start, rank), :vecs],
                preferred_element_type=jnp.float32,
            )
        above = jnp.zeros((rank, vecs), jnp.float32)
        for m in range(top_ref.shape[0]):
            above = above + jnp.dot(
                top_ref[m],
                parents[lax.rem(scalars[1] + 1 + m, clusters)],
                preferred_element_type=jnp.float32,
            )
        field = field + jnp.dot(
            nested_ref[...], above.astype(jnp.bfloat16), preferred_element_type=jnp.float32
        )
        far = jnp.dot(
            basis_ref[...], field.astype(jnp.bfloat16), preferred_element_type=jnp.float32
        )
        row = lax.broadcasted_iota(jnp.int32, (rows, vecs), 0)
        out_ref[...] = jnp.where(row < scalars[0], out_ref[...] + far, 0.0)


def body(
    vectors,
    near_tiles,
    leaf_basis,
    transfer,
    coupling,
    top_coupling,
    near_list,
    far_list,
    row_counts,
):
    leaves = lax.axis_size("leaf")
    clusters = lax.axis_size("top")
    rows, vecs = vectors.shape[2:]
    keep = (jnp.arange(rows, dtype=jnp.int32) < row_counts[0, 0]).astype(jnp.bfloat16)
    masked = vectors[0, 0] * keep[:, None]
    basis = leaf_basis[0, 0]
    nested = transfer[0, 0]
    rank = nested.shape[0]
    coeff = jnp.einsum("ir,iv->rv", basis, masked, preferred_element_type=jnp.float32).astype(
        jnp.bfloat16
    )
    packed = jnp.concatenate([coeff, nested], axis=1)
    tiles = near_tiles[0, 0]
    bits = leaves.bit_length() - 1
    span = 2 * REACH + 1
    vmem = pl.BlockSpec(memory_space=pltpu.VMEM)
    window, gathered, parents = pl.pallas_call(
        functools.partial(kernel, leaves, clusters),
        out_shape=(
            jax.ShapeDtypeStruct((span, rows, vecs), jnp.bfloat16),
            jax.ShapeDtypeStruct((leaves * rank, vecs + rank), jnp.bfloat16),
            jax.ShapeDtypeStruct((clusters, rank, vecs), jnp.bfloat16),
        ),
        in_specs=[vmem, vmem],
        out_specs=(pl.BlockSpec(memory_space=pl.ANY), vmem, vmem),
        scratch_shapes=[
            pltpu.SemaphoreType.DMA((span,)),
            pltpu.SemaphoreType.DMA((span,)),
            pltpu.SemaphoreType.DMA((bits,)),
            pltpu.SemaphoreType.DMA((bits,)),
            pltpu.SemaphoreType.DMA((clusters,)),
            pltpu.SemaphoreType.DMA((clusters,)),
            pltpu.SemaphoreType.DMA,
            pltpu.SemaphoreType.DMA,
        ],
        compiler_params=pltpu.CompilerParams(
            collective_id=0, has_side_effects=True, vmem_limit_bytes=24 * 1024 * 1024
        ),
        cost_estimate=pl.CostEstimate(
            flops=2 * leaves * rank * rank * vecs,
            bytes_accessed=16 * span * rows * vecs,
            transcendentals=0,
        ),
    )(masked, packed)
    me = lax.axis_index("leaf")
    offsets = near_list[0, 0]
    valid = (me + offsets >= 0) & (me + offsets < leaves)
    slots = jnp.where(valid, offsets + REACH, REACH)
    places = mirrored(far_list[0, 0], bits)
    scalars = jnp.stack([row_counts[0, 0], lax.axis_index("top")]).astype(jnp.int32)

    def whole(array):
        return pl.BlockSpec(array.shape, lambda k, *_: (0,) * array.ndim)

    rest = (gathered, parents, basis, nested, coupling[0, 0], top_coupling[0])
    result = pl.pallas_call(
        functools.partial(local_kernel, clusters),
        out_shape=jax.ShapeDtypeStruct((rows, vecs), jnp.float32),
        grid_spec=pltpu.PrefetchScalarGridSpec(
            num_scalar_prefetch=4,
            grid=(tiles.shape[0],),
            in_specs=[
                pl.BlockSpec((1, rows, rows), lambda k, *_: (k, 0, 0)),
                pl.BlockSpec((1, rows, vecs), lambda k, slots, *_: (slots[k], 0, 0)),
            ]
            + [whole(array) for array in rest],
            out_specs=pl.BlockSpec((rows, vecs), lambda k, *_: (0, 0)),
        ),
        compiler_params=pltpu.CompilerParams(
            dimension_semantics=("arbitrary",), vmem_limit_bytes=32 * 1024 * 1024
        ),
    )(slots, valid.astype(jnp.int32), places, scalars, tiles, window, *rest)
    return result[None, None]


def solution(mesh):
    in_specs = (
        P("top", "leaf", None, None),
        P("top", "leaf", None, None, None),
        P("top", "leaf", None, None),
        P("top", "leaf", None, None),
        P("top", "leaf", None, None, None),
        P("top", None, None, None),
        P("top", "leaf", None),
        P("top", "leaf", None),
        P("top", "leaf"),
    )
    out_specs = P("top", "leaf", None, None)
    return jax.shard_map(body, mesh=mesh, in_specs=in_specs, out_specs=out_specs, check_vma=False)
```

profile of v0, /device:TPU:5, one launch (start us, length us, event | category | flops | bytes accessed | tf_op | source)
XLA Modules:
  0.0 85.1 jit_solution(17156552667097526076)
XLA Ops:
  0.7 0.1 pad_add_fusion.scalars
  0.7 0.7 fusion.10.places
  1.4 0.7 select_bitcast_fusion.slots
  2.1 0.7 convert_bitcast_fusion.valid
  2.7 1.6 %fusion = bf16[128,512]{1,0:T(8,128)(2,1)S(1)} fusion(bf16[1,1,768,512]{3,2,1,0:T(8,128)(2,1)} %param.9, bf16[768]{0:T(1024)(128)(2,1)S(1)} %fusion.4, bf16[1,1,768,128]{3,2,1,0:T(8,128)(2,1)} %param.11), kind=kOutput, calls=%fused_computation.1 | convolution fusion | flops 101122048 | bytes 1115648 | tf_op jit(solution)/shard_map/ir,iv->rv/dot_general | solution.py:308
  4.3 0.8 pad_maximum_fusion.packed_ref
  5.1 1.3 %bitcast_multiply_fusion.masked_ref = bf16[768,512]{1,0:T(8,128)(2,1)S(1)} fusion(bf16[1,1,768,512]{3,2,1,0:T(8,128)(2,1)} %param.9, bf16[768]{0:T(1024)(128)(2,1)S(1)} %fusion.4), kind=kLoop, calls=%fused_computation.3 | loop fusion | flops 393216 | bytes 1574400 | tf_op jit(solution)/shard_map/mul | solution.py:304
  6.4 59.7 %shard_map.91 = (bf16[9,768,512]{2,1,0:T(8,128)(2,1)S(1)}, bf16[2048,640]{1,0:T(8,128)(2,1)S(1)}, bf16[2,128,512]{2,1,0:T(8,128)(2,1)S(1)}) custom-call(bf16[768,512]{1,0:T(8,128)(2,1)S(1)} %bitcast_multiply_fusion.masked_ref, bf16[128,640]{1,0:T(8,128)(2,1)S(1)} %pad_maximum_fusion.packed_ref), custom_call_target="tpu_custom_call" | custom-call | flops 268435456 | bytes 56623104 | tf_op jit(solution)/shard_map/pallas_call | solution.py:316
  66.2 0.0 copy-start
  66.2 3.7 %copy-done = bf16[1,1,8,768,768]{4,3,2,1,0:T(8,128)(2,1)S(1)} copy-done((bf16[1,1,8,768,768]{4,3,2,1,0:T(8,128)(2,1)S(1)}, bf16[1,1,8,768,768]{4,3,2,1,0:T(8,128)(2,1)}, u32[]{:S(2)}) %copy-start) | copy-done | bytes 9437208
  69.8 0.0 copy-start.1
  69.8 0.9 %copy-done.1 = bf16[1,1,7,128,128]{4,3,2,1,0:T(8,128)(2,1)S(1)} copy-done((bf16[1,1,7,128,128]{4,3,2,1,0:T(8,128)(2,1)S(1)}, bf16[1,1,7,128,128]{4,3,2,1,0:T(8,128)(2,1)}, u32[]{:S(2)}) %copy-start.1) | copy-done | bytes 229400
  70.8 0.0 copy-start.2
  70.8 0.9 %copy-done.2 = bf16[1,1,768,128]{3,2,1,0:T(8,128)(2,1)S(1)} copy-done((bf16[1,1,768,128]{3,2,1,0:T(8,128)(2,1)S(1)}, bf16[1,1,768,128]{3,2,1,0:T(8,128)(2,1)}, u32[]{:S(2)}) %copy-start.2) | copy-done | bytes 196632
  71.7 0.0 copy-start.3
  71.7 0.8 copy-done.3
  72.5 0.0 copy-start.4
  72.5 0.8 copy-done.4
  73.3 11.8 %shard_map.92 = f32[768,512]{1,0:T(8,128)} custom-call(s32[8]{0:T(128)S(1)} %select_bitcast_fusion.slots, s32[8]{0:T(128)S(1)} %convert_bitcast_fusion.valid, s32[7]{0:T(128)S(1)} %fusion.10.places, s32[2]{0:T(128)S(1)} %pad_add_fusion.scalars, bf16[8,768,768]{2,1,0:T(8,128)(2,1)S(1)} %bitcast.37, bf16[9,768,512]{2,1,0:T(8,128)(2,1)S(1)} %get-tuple-element.8.source_ref, ...), custom_call_target="tpu_custom_call" | custom-call | tf_op jit(solution)/shard_map/pallas_call | solution.py:355
  (1 shorter events, 0.0 us)
Async XLA Ops:
  66.2 3.7 %copy-start = (bf16[1,1,8,768,768]{4,3,2,1,0:T(8,128)(2,1)S(1)}, bf16[1,1,8,768,768]{4,3,2,1,0:T(8,128)(2,1)}, u32[]{:S(2)}) copy-start(bf16[1,1,8,768,768]{4,3,2,1,0:T(8,128)(2,1)} %param.10) | copy-start | bytes 28311556
  69.8 0.9 %copy-start.1 = (bf16[1,1,7,128,128]{4,3,2,1,0:T(8,128)(2,1)S(1)}, bf16[1,1,7,128,128]{4,3,2,1,0:T(8,128)(2,1)}, u32[]{:S(2)}) copy-start(bf16[1,1,7,128,128]{4,3,2,1,0:T(8,128)(2,1)} %param.13) | copy-start | bytes 688132
  70.8 0.9 %copy-start.2 = (bf16[1,1,768,128]{3,2,1,0:T(8,128)(2,1)S(1)}, bf16[1,1,768,128]{3,2,1,0:T(8,128)(2,1)}, u32[]{:S(2)}) copy-start(bf16[1,1,768,128]{3,2,1,0:T(8,128)(2,1)} %param.11) | copy-start | bytes 589828
  71.7 0.8 copy-start.3
  72.5 0.8 copy-start.4
where the time goes:
time: 86.6 us; the launch traced here: 85.1 us
  Pallas kernels  71.6 us (83%)
  local copies, waits for them, and re-layouts  7.14 us (8%)
  other arithmetic  4.15 us (5%)
  matrix products  1.58 us (2%)
    pallas_call x1, Pallas kernels, body(): pl.pallas_call(functools.partial(kernel, leaves, clusters), out_shape=(ja...  59.7 us
    pallas_call x1, Pallas kernels, body(): pl.pallas_call(functools.partial(local_kernel, clusters), out_shape=jax.S...  11.8 us
    unnamed x10, local copies, waits for them, and re-layouts  7.14 us

commit v1 on v0

v1 whole, which is shorter than its diff:
```python
import functools

import jax
import jax.numpy as jnp
from jax import lax
from jax.experimental import pallas as pl
from jax.experimental.pallas import tpu as pltpu
from jax.sharding import PartitionSpec as P

REACH = 4
SLOTS = 2 * REACH + 2
PIECES = 3


def contract(left, right):
    return lax.dot_general(left, right, (((0,), (0,)), ((), ())), preferred_element_type=jnp.float32)


def dot(left, right):
    return jnp.dot(left, right, preferred_element_type=jnp.float32)


def send_count(levels, clusters):
    return 40 + 12 * levels + clusters


def exchange_kernel(
    levels,
    clusters,
    near_ref,
    far_ref,
    count_ref,
    vectors_ref,
    tiles_ref,
    basis_ref,
    nested_ref,
    coupling_ref,
    top_ref,
    acc,
    field_ref,
    raw,
    tiles,
    basis,
    nested,
    coupling,
    top,
    window,
    coeffs,
    halves,
    half_in,
    quarters,
    partial,
    quarter_in,
    sums,
    parents,
    fields,
    tile_sem,
    load_sem,
    send_sem,
    block_sem,
    piece_sem,
    coeff_sem,
    half_sem,
    quarter_sem,
    sum_sem,
    parent_sem,
    field_sem,
):
    me = lax.axis_index("leaf")
    cluster = lax.axis_index("top")
    core = lax.rem(me, 2)
    column = lax.rem(lax.div(me, 2), 2)
    level = lax.div(me, 4)
    other = 1 - core
    partner = me + 1 - 2 * core
    beside = me + 2 - 4 * column
    above = level < levels - 1
    below = level > 0
    first_column = column == 0
    rows, vecs = raw.shape
    half = vecs // 2
    quarter = vecs // 4
    piece = rows // PIECES
    tile_count = tiles.shape[0]

    def load(source, target, sem):
        return pltpu.make_async_copy(source, target, sem)

    raw_load = load(vectors_ref.at[0, 0], raw, load_sem.at[0])
    basis_load = load(basis_ref.at[0, 0], basis, load_sem.at[1])
    nested_load = load(nested_ref.at[0, 0], nested, load_sem.at[2])
    coupling_load = load(coupling_ref.at[0, 0], coupling, load_sem.at[3])
    top_load = load(top_ref.at[0], top, load_sem.at[4])
    tile_loads = [load(tiles_ref.at[0, 0, k], tiles.at[k], tile_sem.at[k]) for k in range(tile_count)]
    for copy in [raw_load, basis_load, nested_load] + tile_loads + [coupling_load, top_load]:
        copy.start()

    barrier = pltpu.get_barrier_semaphore()
    peers = [{"leaf": partner}, {"leaf": beside}]
    for step in range(1, levels):
        peers.append({"leaf": lax.rem(me + 4 * step, 4 * levels)})
    for step in range(1, clusters):
        peers.append({"top": lax.rem(cluster + step, clusters)})
    for peer in peers:
        pl.semaphore_signal(barrier, inc=1, device_id=peer, device_id_type=pl.DeviceIdType.MESH)

    sent = []

    def send(source, target, sem, peer, condition=None):
        copy = pltpu.make_async_remote_copy(
            src_ref=source,
            dst_ref=target,
            send_sem=send_sem.at[len(sent)],
            recv_sem=sem,
            device_id=peer,
            device_id_type=pl.DeviceIdType.MESH,
        )
        sent.append((condition, copy))
        if condition is None:
            copy.start()
        else:
            pl.when(condition)(copy.start)

    def receive(block, sem, condition=None):
        copy = pltpu.make_async_remote_copy(
            src_ref=block,
            dst_ref=block,
            send_sem=send_sem.at[0],
            recv_sem=sem,
            device_id={"leaf": partner},
            device_id_type=pl.DeviceIdType.MESH,
        )
        if condition is None:
            copy.wait_recv()
        else:
            pl.when(condition)(copy.wait_recv)

    to_partner, to_beside = {"leaf": partner}, {"leaf": beside}
    to_above, to_below = {"leaf": me + 4}, {"leaf": me - 4}

    own_slot = REACH + core
    partner_slot = REACH + other
    beside_slot = core + 6 - 4 * column
    diagonal_slot = core + 2 + 4 * column
    below_slot = core
    above_slot = core + 8
    diagonal = jnp.logical_or(
        jnp.logical_and(first_column, below), jnp.logical_and(column == 1, above)
    )
    relay_over = jnp.logical_or(
        jnp.logical_and(column == 1, below), jnp.logical_and(first_column, above)
    )
    relay_up = jnp.logical_and(first_column, above)
    relay_down = jnp.logical_and(column == 1, below)

    def send_block(slot, part, target, peer, condition=None):
        send(window.at[slot, part], window.at[target, part], block_sem.at[target, part], peer, condition)

    def wait_block(slot, part, condition=None):
        receive(window.at[slot, part], block_sem.at[slot, part], condition)

    def span_of(index):
        return pl.ds(index * piece, piece)

    def send_piece(slot, part, index, target, peer, condition=None):
        send(
            window.at[slot, part, span_of(index)],
            window.at[target, part, span_of(index)],
            piece_sem.at[target, part, index],
            peer,
            condition,
        )

    def wait_piece(slot, part, index, condition=None):
        receive(window.at[slot, part, span_of(index)], piece_sem.at[slot, part, index], condition)

    def send_coeff(leaf, peer, condition=None):
        send(coeffs.at[leaf], coeffs.at[leaf], coeff_sem.at[leaf], peer, condition)

    def wait_coeff(leaf, condition=None):
        receive(coeffs.at[leaf], coeff_sem.at[leaf], condition)

    def exists(step):
        return jnp.logical_and(level + step >= 0, level + step < levels)

    def crosses(step, from_first):
        return step <= -1 or step >= 2 if from_first else step >= 1 or step <= -2

    def crossing(step):
        if crosses(step, True) and crosses(step, False):
            return exists(step)
        return jnp.logical_and(exists(step), first_column if crosses(step, True) else column == 1)

    def crossed(step):
        if crosses(step, True) and crosses(step, False):
            return exists(step)
        return jnp.logical_and(exists(step), column == 1 if crosses(step, True) else first_column)

    def handed(step, which):
        if abs(step) >= 2:
            return exists(step)
        return jnp.logical_and(exists(step), which == (1 if step == 1 else 0))

    def relay_coeffs(hop):
        for step in (-hop, hop):
            wait_coeff(me + 4 * step, exists(step))
        if hop + 1 < levels:
            send_coeff(me - 4 * hop, to_above, jnp.logical_and(exists(-hop), above))
            send_coeff(me + 4 * hop, to_below, jnp.logical_and(exists(hop), below))

    def cross_coeffs(hop):
        for step in (-hop, hop):
            send_coeff(me + 4 * step, to_beside, crossing(step))
            send_coeff(me + 4 * step, to_partner, handed(step, core))

    def hand_crossed(hop):
        for step in (-hop, hop):
            wait_coeff(beside + 4 * step, crossed(step))
            send_coeff(beside + 4 * step, to_partner, crossed(step))

    def near(slot, part, condition=None, first=False, index=None):
        offset = slot - REACH - core
        place, hit = 0, 0
        for k in range(tile_count):
            here = near_ref[0, 0, k] == offset
            place = jnp.where(here, k, place)
            hit = jnp.where(here, 1, hit)
        scale = hit.astype(jnp.float32)

        def run():
            def step(block, carry):
                span = pl.ds(pl.multiple_of(block * piece, piece), piece)
                if index is None:
                    product = dot(tiles[place, span, :], window[slot, part])
                else:
                    product = dot(
                        tiles[place, span, index * piece : (index + 1) * piece],
                        window[slot, part, index * piece : (index + 1) * piece, :],
                    )
                if first:
                    acc[part, span, :] = product * scale
                else:
                    acc[part, span, :] += product * scale
                return carry

            lax.fori_loop(0, PIECES, step, 0)

        if condition is None:
            run()
        else:
            pl.when(condition)(run)

    raw_load.wait()
    live = lax.broadcasted_iota(jnp.int32, (rows, half), 0) < count_ref[0, 0]
    basis_load.wait()
    for part in range(2):
        columns = slice(part * half, (part + 1) * half)
        masked = jnp.where(live, raw[:, columns], jnp.zeros((), jnp.bfloat16))
        window[own_slot, part] = masked
        coeffs[me, :, columns] = contract(basis[...], masked).astype(jnp.bfloat16)
    nested_load.wait()
    for part in range(2):
        halves[part] = contract(nested[...], coeffs[me, :, part * half : (part + 1) * half])
    pl.semaphore_wait(barrier, len(peers))

    send_coeff(me, to_above, above)
    send_coeff(me, to_below, below)
    send(halves.at[other], half_in, half_sem.at[0], to_partner)
    for index in range(PIECES - 1):
        send_piece(own_slot, 0, index, own_slot + 4 * column - 2, to_beside)
    send_block(own_slot, 0, core, to_above, above)
    send_block(own_slot, 0, core + 8, to_below, below)
    for part in range(2):
        send_block(own_slot, part, own_slot, to_partner)

    receive(half_in, half_sem.at[0])
    total = halves[core] + half_in[...]
    for part in range(2):
        value = total[:, part * quarter : (part + 1) * quarter]
        partial[part] = value
        quarters[part] = value.astype(jnp.bfloat16)
    for copy in tile_loads:
        copy.wait()
    near(own_slot, 0, first=True)
    send(quarters.at[1 - column], quarter_in, quarter_sem.at[0], to_beside)
    send_piece(own_slot, 0, PIECES - 1, own_slot + 4 * column - 2, to_beside)
    near(own_slot, 1, first=True)
    for part in range(2):
        wait_block(partner_slot, part)
        near(partner_slot, part)

    relay_coeffs(1)
    cross_coeffs(1)
    send_block(own_slot, 1, own_slot + 4 * column - 2, to_beside)
    receive(quarter_in, quarter_sem.at[0])
    sums[level] = (partial[column] + quarter_in[...].astype(jnp.float32)).astype(jnp.bfloat16)
    send_sums = []
    for step in range(1, levels):
        send_sums.append(lax.rem(me + 4 * step, 4 * levels))
    for leaf in send_sums:
        send(sums.at[level], sums.at[level], sum_sem.at[level], {"leaf": leaf})
    send_block(own_slot, 1, core, to_above, above)
    send_block(own_slot, 1, core + 8, to_below, below)

    bridged_slot = jnp.where(core == 0, 1, 8)
    bridged = jnp.logical_or(
        jnp.logical_and(core == 0, below), jnp.logical_and(core == 1, above)
    )
    hand_below = jnp.logical_and(core == 1, below)
    hand_above = jnp.logical_and(core == 0, above)
    far_beside_slot = other + 6 - 4 * column
    far_diagonal_slot = other + 2 + 4 * column

    def hand_neighbours(part):
        send_block(below_slot, part, below_slot, to_partner, hand_below)
        send_block(above_slot, part, above_slot, to_partner, hand_above)

    for index in range(PIECES):
        wait_piece(beside_slot, 0, index)
    send_block(beside_slot, 0, beside_slot, to_partner)
    near(beside_slot, 0)
    wait_block(below_slot, 0, below)
    wait_block(above_slot, 0, above)
    hand_neighbours(0)
    near(below_slot, 0, below)
    near(above_slot, 0, above)

    hand_crossed(1)
    if levels > 2:
        relay_coeffs(2)
        cross_coeffs(2)
    for step in range(1, levels):
        source = lax.rem(level + step, levels)
        receive(sums.at[source], sum_sem.at[source])
    whole = sums[0].astype(jnp.float32)
    for index in range(1, levels):
        whole = whole + sums[index].astype(jnp.float32)
    parents[cluster] = whole.astype(jnp.bfloat16)
    for step in range(1, clusters):
        send(
            parents.at[cluster],
            parents.at[cluster],
            parent_sem.at[cluster],
            {"top": lax.rem(cluster + step, clusters)},
        )
    wait_block(far_beside_slot, 0)
    near(far_beside_slot, 0)
    wait_block(bridged_slot, 0, bridged)
    near(bridged_slot, 0, bridged)

    coupling_load.wait()
    top_load.wait()
    for step in range(1, clusters):
        source = lax.rem(cluster + step, clusters)
        receive(parents.at[source], parent_sem.at[source])
    over = jnp.zeros(parents.shape[1:], jnp.float32)
    for m in range(top.shape[0]):
        over = over + dot(top[m], parents[lax.rem(cluster + 1 + m, clusters)])
    place = 2 * core + column
    fields[place] = over.astype(jnp.bfloat16)
    send(fields.at[place], fields.at[place], field_sem.at[place], to_beside)
    send_block(below_slot, 0, core + 2, to_beside, relay_down)
    send_block(above_slot, 0, core + 6, to_beside, relay_up)

    wait_block(beside_slot, 1)
    for index in range(PIECES):
        send_piece(beside_slot, 1, index, core + 2, to_above, relay_up)
        send_piece(beside_slot, 1, index, core + 6, to_below, relay_down)
    send_block(beside_slot, 1, beside_slot, to_partner)
    near(beside_slot, 1)
    wait_block(below_slot, 1, below)
    wait_block(above_slot, 1, above)
    hand_neighbours(1)
    near(below_slot, 1, below)
    near(above_slot, 1, above)
    if levels > 2:
        hand_crossed(2)
    for hop in range(3, levels):
        relay_coeffs(hop)
        cross_coeffs(hop)
    next_place = 2 * core + 1 - column
    receive(fields.at[next_place], field_sem.at[next_place])
    pair = fields.at[pl.ds(2 * core, 2)]
    send(pair, pair, field_sem.at[4 + core], to_partner)
    wait_block(far_beside_slot, 1)
    near(far_beside_slot, 1)
    wait_block(bridged_slot, 1, bridged)
    near(bridged_slot, 1, bridged)

    wait_block(diagonal_slot, 0, diagonal)
    send_block(diagonal_slot, 0, diagonal_slot, to_partner, diagonal)
    near(diagonal_slot, 0, diagonal)
    wait_block(far_diagonal_slot, 0, diagonal)
    near(far_diagonal_slot, 0, diagonal)
    for hop in range(3, levels):
        hand_crossed(hop)
    for index in range(PIECES):
        wait_piece(diagonal_slot, 1, index, diagonal)
        send_piece(diagonal_slot, 1, index, diagonal_slot, to_partner, diagonal)
        near(diagonal_slot, 1, diagonal, index=index)
        if index > 0:
            wait_piece(far_diagonal_slot, 1, index - 1, diagonal)
            near(far_diagonal_slot, 1, diagonal, index=index - 1)

    for hop in range(1, levels):
        for step in (-hop, hop):
            wait_coeff(partner + 4 * step, handed(step, other))
            wait_coeff(beside + 1 - 2 * core + 4 * step, crossed(step))
    theirs = fields.at[pl.ds(2 * other, 2)]
    receive(theirs, field_sem.at[4 + other])
    field = dot(nested[...], jnp.concatenate([fields[k] for k in range(4)], axis=1))
    for m in range(coupling.shape[0]):
        field = field + dot(coupling[m], coeffs[far_ref[0, 0, m]])
    field_ref[...] = field.astype(jnp.bfloat16)
    wait_piece(far_diagonal_slot, 1, PIECES - 1, diagonal)
    near(far_diagonal_slot, 1, diagonal, index=PIECES - 1)

    for condition, copy in sent:
        if condition is None:
            copy.wait_send()
        else:
            pl.when(condition)(copy.wait_send)


def finish_kernel(count_ref, acc_ref, field_ref, basis_ref, out_ref):
    rows, vecs = out_ref.shape
    half = vecs // 2
    row = lax.broadcasted_iota(jnp.int32, (rows, half), 0) + pl.program_id(0) * rows
    live = row < count_ref[0, 0]
    for part in range(2):
        columns = slice(part * half, (part + 1) * half)
        value = acc_ref[part] + dot(basis_ref[0, 0], field_ref[:, columns])
        out_ref[:, columns] = jnp.where(live, value, 0.0)


def body(
    vectors,
    near_tiles,
    leaf_basis,
    transfer,
    coupling,
    top_coupling,
    near_list,
    far_list,
    row_counts,
):
    leaves = lax.axis_size("leaf")
    clusters = lax.axis_size("top")
    levels = leaves // 4
    rows, vecs = vectors.shape[2:]
    rank = transfer.shape[2]
    half, quarter = vecs // 2, vecs // 4
    smem = pl.BlockSpec(memory_space=pltpu.SMEM)
    vmem = pl.BlockSpec(memory_space=pltpu.VMEM)
    hbm = pl.BlockSpec(memory_space=pltpu.HBM)
    dma = pltpu.SemaphoreType.DMA
    acc, field = pl.pallas_call(
        functools.partial(exchange_kernel, levels, clusters),
        out_shape=(
            jax.ShapeDtypeStruct((2, rows, half), jnp.float32),
            jax.ShapeDtypeStruct((rank, vecs), jnp.bfloat16),
        ),
        in_specs=[smem] * 3 + [hbm] * 6,
        out_specs=(vmem, vmem),
        scratch_shapes=[
            pltpu.VMEM((rows, vecs), jnp.bfloat16),
            pltpu.VMEM(near_tiles.shape[2:], jnp.bfloat16),
            pltpu.VMEM(leaf_basis.shape[2:], jnp.bfloat16),
            pltpu.VMEM(transfer.shape[2:], jnp.bfloat16),
            pltpu.VMEM(coupling.shape[2:], jnp.bfloat16),
            pltpu.VMEM(top_coupling.shape[1:], jnp.bfloat16),
            pltpu.VMEM((SLOTS, 2, rows, half), jnp.bfloat16),
            pltpu.VMEM((leaves, rank, vecs), jnp.bfloat16),
            pltpu.VMEM((2, rank, half), jnp.float32),
            pltpu.VMEM((rank, half), jnp.float32),
            pltpu.VMEM((2, rank, quarter), jnp.bfloat16),
            pltpu.VMEM((2, rank, quarter), jnp.float32),
            pltpu.VMEM((rank, quarter), jnp.bfloat16),
            pltpu.VMEM((levels, rank, quarter), jnp.bfloat16),
            pltpu.VMEM((clusters, rank, quarter), jnp.bfloat16),
            pltpu.VMEM((4, rank, quarter), jnp.bfloat16),
            dma((near_tiles.shape[2],)),
            dma((5,)),
            dma((send_count(levels, clusters),)),
            dma((SLOTS, 2)),
            dma((SLOTS, 2, PIECES)),
            dma((leaves,)),
            dma((1,)),
            dma((1,)),
            dma((levels,)),
            dma((clusters,)),
            dma((6,)),
        ],
        compiler_params=pltpu.CompilerParams(
            collective_id=0, has_side_effects=True, vmem_limit_bytes=62 * 1024 * 1024
        ),
    )(
        near_list,
        far_list,
        row_counts,
        vectors,
        near_tiles,
        leaf_basis,
        transfer,
        coupling,
        top_coupling,
    )
    steps = PIECES
    result = pl.pallas_call(
        finish_kernel,
        out_shape=jax.ShapeDtypeStruct((rows, vecs), jnp.float32),
        grid=(steps,),
        in_specs=[
            smem,
            pl.BlockSpec((2, rows // steps, half), lambda i: (0, i, 0)),
            pl.BlockSpec((rank, vecs), lambda i: (0, 0)),
            pl.BlockSpec((1, 1, rows // steps, rank), lambda i: (0, 0, i, 0)),
        ],
        out_specs=pl.BlockSpec((rows // steps, vecs), lambda i: (i, 0)),
        compiler_params=pltpu.CompilerParams(
            dimension_semantics=("arbitrary",), vmem_limit_bytes=12 * 1024 * 1024
        ),
    )(row_counts, acc, field, leaf_basis)
    return result[None, None]


def solution(mesh):
    in_specs = (
        P("top", "leaf", None, None),
        P("top", "leaf", None, None, None),
        P("top", "leaf", None, None),
        P("top", "leaf", None, None),
        P("top", "leaf", None, None, None),
        P("top", None, None, None),
        P("top", "leaf", None),
        P("top", "leaf", None),
        P("top", "leaf"),
    )
    out_specs = P("top", "leaf", None, None)
    return jax.shard_map(body, mesh=mesh, in_specs=in_specs, out_specs=out_specs, check_vma=False)
```

time: 86.6 us -> 53.7 us (0.62)
  the two profiles are of different devices: /device:TPU:5 before, /device:TPU:17 now
where the time goes in v1:
time: 53.7 us; the launch traced here: 53.5 us
  Pallas kernels  50.5 us (94%)
  local copies, waits for them, and re-layouts  2.31 us (4%)
  between operations  0.69 us (1%)
    pallas_call x1, Pallas kernels, body(): pl.pallas_call(functools.partial(exchange_kernel, levels, clusters), out_...  48.4 us
    unnamed x6, local copies, waits for them, and re-layouts  2.31 us
    pallas_call x1, Pallas kernels, body(): pl.pallas_call(finish_kernel, out_shape=jax.ShapeDtypeStruct((rows, vecs)...  2.11 us

profile of v1, /device:TPU:17, one launch (start us, length us, event | category | flops | bytes accessed | tf_op | source)
XLA Modules:
  0.0 53.5 jit_solution(12334788134309691789)
XLA Ops:
  0.7 0.0 copy-start.1
  0.7 48.4 %shard_map.91 = (f32[2,768,256]{2,1,0:T(8,128)}, bf16[128,512]{1,0:T(8,128)(2,1)}) custom-call(s32[1,1,8]{2,1,0:T(1,128)} %near_ref.1, s32[1,1,7]{2,1,0:T(1,128)} %far_ref.1, s32[1,1]{1,0:T(1,128)S(6)} %copy.10.count_ref, bf16[1,1,768,512]{3,2,1,0:T(8,128)(2,1)} %vectors_ref.1, bf16[1,1,8,768,768]{4,3,2,1,0:T(8,128)(2,1)} %tiles_ref.1, ...), custom_call_target="tpu_custom_call" | custom-call | tf_op jit(solution)/shard_map/pallas_call | solution.py:457
  49.1 0.0 copy-done.1
  49.1 0.0 copy-start
  49.1 1.4 %copy-done = f32[2,768,256]{2,1,0:T(8,128)S(1)} copy-done((f32[2,768,256]{2,1,0:T(8,128)S(1)}, f32[2,768,256]{2,1,0:T(8,128)}, u32[]{:S(2)}) %copy-start) | copy-done | bytes 1572888
  50.5 0.0 copy-start.2
  50.5 0.9 %copy-done.2 = bf16[128,512]{1,0:T(8,128)(2,1)S(1)} copy-done((bf16[128,512]{1,0:T(8,128)(2,1)S(1)}, bf16[128,512]{1,0:T(8,128)(2,1)}, u32[]{:S(2)}) %copy-start.2) | copy-done | bytes 131096
  51.4 2.1 %shard_map.92 = f32[768,512]{1,0:T(8,128)} custom-call(s32[1,1]{1,0:T(1,128)S(6)} %copy.10.count_ref, f32[2,768,256]{2,1,0:T(8,128)S(1)} %copy-done, bf16[128,512]{1,0:T(8,128)(2,1)S(1)} %copy-done.2, bf16[1,1,768,128]{3,2,1,0:T(8,128)(2,1)S(1)} %copy-done.1), custom_call_target="tpu_custom_call" | custom-call | tf_op jit(solution)/shard_map/pallas_call | solution.py:509
Async XLA Ops:
  0.7 48.4 %copy-start.1 = (bf16[1,1,768,128]{3,2,1,0:T(8,128)(2,1)S(1)}, bf16[1,1,768,128]{3,2,1,0:T(8,128)(2,1)}, u32[]{:S(2)}) copy-start(bf16[1,1,768,128]{3,2,1,0:T(8,128)(2,1)} %basis_ref.3) | copy-start | bytes 589828
  49.1 1.4 %copy-start = (f32[2,768,256]{2,1,0:T(8,128)S(1)}, f32[2,768,256]{2,1,0:T(8,128)}, u32[]{:S(2)}) copy-start(f32[2,768,256]{2,1,0:T(8,128)} %get-tuple-element.7.acc_ref) | copy-start | bytes 4718596
  50.5 0.9 %copy-start.2 = (bf16[128,512]{1,0:T(8,128)(2,1)S(1)}, bf16[128,512]{1,0:T(8,128)(2,1)}, u32[]{:S(2)}) copy-start(bf16[128,512]{1,0:T(8,128)(2,1)} %get-tuple-element.8.field_ref) | copy-start | bytes 393220

commit v2 on v1

--- a/solution.py
+++ b/solution.py
@@ -27,9 +27,9 @@
 def exchange_kernel(
     levels,
     clusters,
-    near_ref,
-    far_ref,
     count_ref,
+    near_source,
+    far_source,
     vectors_ref,
     tiles_ref,
     basis_ref,
@@ -38,6 +38,8 @@
     top_ref,
     acc,
     field_ref,
+    near_ref,
+    far_ref,
     raw,
     tiles,
     basis,
@@ -51,7 +53,8 @@
     quarters,
     partial,
     quarter_in,
-    sums,
+    line_out,
+    line_in,
     parents,
     fields,
     tile_sem,
@@ -62,7 +65,7 @@
     coeff_sem,
     half_sem,
     quarter_sem,
-    sum_sem,
+    line_sem,
     parent_sem,
     field_sem,
 ):
@@ -92,17 +95,24 @@
     coupling_load = load(coupling_ref.at[0, 0], coupling, load_sem.at[3])
     top_load = load(top_ref.at[0], top, load_sem.at[4])
     tile_loads = [load(tiles_ref.at[0, 0, k], tiles.at[k], tile_sem.at[k]) for k in range(tile_count)]
-    for copy in [raw_load, basis_load, nested_load] + tile_loads + [coupling_load, top_load]:
+    near_load = load(near_source, near_ref, load_sem.at[5])
+    far_load = load(far_source, far_ref, load_sem.at[6])
+
+    barrier = pltpu.get_barrier_semaphore()
+
+    def greet(peer):
+        pl.semaphore_signal(barrier, inc=1, device_id=peer, device_id_type=pl.DeviceIdType.MESH)
+
+    greet({"leaf": partner})
+    greet({"leaf": beside})
+    for step in range(1, clusters):
+        greet({"top": lax.rem(cluster + step, clusters)})
+    pl.when(above)(lambda: greet({"leaf": me + 4}))
+    pl.when(below)(lambda: greet({"leaf": me - 4}))
+    expected = clusters + 1 + above.astype(jnp.int32) + below.astype(jnp.int32)
+    loads = [raw_load, basis_load, nested_load, near_load]
+    for copy in loads + tile_loads + [far_load, coupling_load, top_load]:
         copy.start()
-
-    barrier = pltpu.get_barrier_semaphore()
-    peers = [{"leaf": partner}, {"leaf": beside}]
-    for step in range(1, levels):
-        peers.append({"leaf": lax.rem(me + 4 * step, 4 * levels)})
-    for step in range(1, clusters):
-        peers.append({"top": lax.rem(cluster + step, clusters)})
-    for peer in peers:
-        pl.semaphore_signal(barrier, inc=1, device_id=peer, device_id_type=pl.DeviceIdType.MESH)
 
     sent = []
 
@@ -228,22 +238,15 @@
         scale = hit.astype(jnp.float32)
 
         def run():
-            def step(block, carry):
-                span = pl.ds(pl.multiple_of(block * piece, piece), piece)
-                if index is None:
-                    product = dot(tiles[place, span, :], window[slot, part])
-                else:
-                    product = dot(
-                        tiles[place, span, index * piece : (index + 1) * piece],
-                        window[slot, part, index * piece : (index + 1) * piece, :],
-                    )
-                if first:
-                    acc[part, span, :] = product * scale
-                else:
-                    acc[part, span, :] += product * scale
-                return carry
-
-            lax.fori_loop(0, PIECES, step, 0)
+            if index is None:
+                product = dot(tiles[place], window[slot, part]) * scale
+            else:
+                span = slice(index * piece, (index + 1) * piece)
+                product = dot(tiles[place, :, span], window[slot, part, span, :]) * scale
+            if first:
+                acc[part] = product
+            else:
+                acc[part] += product
 
         if condition is None:
             run()
@@ -261,17 +264,22 @@
     nested_load.wait()
     for part in range(2):
         halves[part] = contract(nested[...], coeffs[me, :, part * half : (part + 1) * half])
-    pl.semaphore_wait(barrier, len(peers))
-
+    pl.semaphore_wait(barrier, expected)
+
+    own_beside = own_slot + 4 * column - 2
     send_coeff(me, to_above, above)
     send_coeff(me, to_below, below)
     send(halves.at[other], half_in, half_sem.at[0], to_partner)
     for index in range(PIECES - 1):
-        send_piece(own_slot, 0, index, own_slot + 4 * column - 2, to_beside)
+        send_piece(own_slot, 0, index, own_beside, to_beside)
     send_block(own_slot, 0, core, to_above, above)
     send_block(own_slot, 0, core + 8, to_below, below)
     for part in range(2):
         send_block(own_slot, part, own_slot, to_partner)
+
+    def send_own(index):
+        send_piece(own_slot, 1, index, core, to_above, above)
+        send_piece(own_slot, 1, index, core + 8, to_below, below)
 
     receive(half_in, half_sem.at[0])
     total = halves[core] + half_in[...]
@@ -279,11 +287,11 @@
         value = total[:, part * quarter : (part + 1) * quarter]
         partial[part] = value
         quarters[part] = value.astype(jnp.bfloat16)
-    for copy in tile_loads:
+    send(quarters.at[1 - column], quarter_in, quarter_sem.at[0], to_beside)
+    send_piece(own_slot, 0, PIECES - 1, own_beside, to_beside)
+    for copy in [near_load] + tile_loads:
         copy.wait()
     near(own_slot, 0, first=True)
-    send(quarters.at[1 - column], quarter_in, quarter_sem.at[0], to_beside)
-    send_piece(own_slot, 0, PIECES - 1, own_slot + 4 * column - 2, to_beside)
     near(own_slot, 1, first=True)
     for part in range(2):
         wait_block(partner_slot, part)
@@ -291,16 +299,28 @@
 
     relay_coeffs(1)
     cross_coeffs(1)
-    send_block(own_slot, 1, own_slot + 4 * column - 2, to_beside)
+    send_block(own_slot, 1, own_beside, to_beside)
     receive(quarter_in, quarter_sem.at[0])
-    sums[level] = (partial[column] + quarter_in[...].astype(jnp.float32)).astype(jnp.bfloat16)
-    send_sums = []
-    for step in range(1, levels):
-        send_sums.append(lax.rem(me + 4 * step, 4 * levels))
-    for leaf in send_sums:
-        send(sums.at[level], sums.at[level], sum_sem.at[level], {"leaf": leaf})
-    send_block(own_slot, 1, core, to_above, above)
-    send_block(own_slot, 1, core + 8, to_below, below)
+    partial[column] += quarter_in[...].astype(jnp.float32)
+
+    def line(turn):
+        for way, at, step in ((0, turn - 1, 4), (1, levels - turn, -4)):
+            here = level == at
+            if turn > 1:
+                receive(line_in.at[way], line_sem.at[way], here)
+            if turn < levels:
+
+                @pl.when(here)
+                def _(way=way):
+                    value = partial[column]
+                    if turn > 1:
+                        value = value + line_in[way].astype(jnp.float32)
+                    line_out[way] = value.astype(jnp.bfloat16)
+
+                send(line_out.at[way], line_in.at[way], line_sem.at[way], {"leaf": me + step}, here)
+
+    line(1)
+    send_own(0)
 
     bridged_slot = jnp.where(core == 0, 1, 8)
     bridged = jnp.logical_or(
@@ -314,6 +334,10 @@
     def hand_neighbours(part):
         send_block(below_slot, part, below_slot, to_partner, hand_below)
         send_block(above_slot, part, above_slot, to_partner, hand_above)
+
+    def send_over(index):
+        send_piece(below_slot, 0, index, core + 2, to_beside, relay_down)
+        send_piece(above_slot, 0, index, core + 6, to_beside, relay_up)
 
     for index in range(PIECES):
         wait_piece(beside_slot, 0, index)
@@ -324,17 +348,34 @@
     hand_neighbours(0)
     near(below_slot, 0, below)
     near(above_slot, 0, above)
+    line(2)
+    send_own(1)
 
     hand_crossed(1)
     if levels > 2:
         relay_coeffs(2)
         cross_coeffs(2)
-    for step in range(1, levels):
-        source = lax.rem(level + step, levels)
-        receive(sums.at[source], sum_sem.at[source])
-    whole = sums[0].astype(jnp.float32)
-    for index in range(1, levels):
-        whole = whole + sums[index].astype(jnp.float32)
+    send_over(0)
+    send_over(1)
+    wait_block(far_beside_slot, 0)
+    near(far_beside_slot, 0)
+    wait_block(bridged_slot, 0, bridged)
+    near(bridged_slot, 0, bridged)
+    for turn in range(3, levels):
+        line(turn)
+    send_own(2)
+
+    wait_block(beside_slot, 1)
+    for index in range(PIECES):
+        send_piece(beside_slot, 1, index, core + 2, to_above, relay_up)
+        send_piece(beside_slot, 1, index, core + 6, to_below, relay_down)
+    send_block(beside_slot, 1, beside_slot, to_partner)
+    near(beside_slot, 1)
+    if levels > 2:
+        line(levels)
+    whole = partial[column]
+    for way, condition in ((0, below), (1, above)):
+        whole = whole + jnp.where(condition, line_in[way].astype(jnp.float32), 0.0)
     parents[cluster] = whole.astype(jnp.bfloat16)
     for step in range(1, clusters):
         send(
@@ -343,11 +384,8 @@
             parent_sem.at[cluster],
             {"top": lax.rem(cluster + step, clusters)},
         )
-    wait_block(far_beside_slot, 0)
-    near(far_beside_slot, 0)
-    wait_block(bridged_slot, 0, bridged)
-    near(bridged_slot, 0, bridged)
-
+    wait_block(far_beside_slot, 1)
+    near(far_beside_slot, 1)
     coupling_load.wait()
     top_load.wait()
     for step in range(1, clusters):
@@ -359,48 +397,48 @@
     place = 2 * core + column
     fields[place] = over.astype(jnp.bfloat16)
     send(fields.at[place], fields.at[place], field_sem.at[place], to_beside)
-    send_block(below_slot, 0, core + 2, to_beside, relay_down)
-    send_block(above_slot, 0, core + 6, to_beside, relay_up)
-
-    wait_block(beside_slot, 1)
-    for index in range(PIECES):
-        send_piece(beside_slot, 1, index, core + 2, to_above, relay_up)
-        send_piece(beside_slot, 1, index, core + 6, to_below, relay_down)
-    send_block(beside_slot, 1, beside_slot, to_partner)
-    near(beside_slot, 1)
-    wait_block(below_slot, 1, below)
-    wait_block(above_slot, 1, above)
-    hand_neighbours(1)
-    near(below_slot, 1, below)
-    near(above_slot, 1, above)
+    send_over(2)
     if levels > 2:
         hand_crossed(2)
     for hop in range(3, levels):
         relay_coeffs(hop)
         cross_coeffs(hop)
+    for index in range(PIECES):
+        wait_piece(below_slot, 1, index, below)
+        wait_piece(above_slot, 1, index, above)
+    hand_neighbours(1)
+    near(below_slot, 1, below)
+    near(above_slot, 1, above)
     next_place = 2 * core + 1 - column
     receive(fields.at[next_place], field_sem.at[next_place])
     pair = fields.at[pl.ds(2 * core, 2)]
     send(pair, pair, field_sem.at[4 + core], to_partner)
-    wait_block(far_beside_slot, 1)
-    near(far_beside_slot, 1)
+
+    def hand_diagonal(part, index):
+        wait_piece(diagonal_slot, part, index, diagonal)
+        send_piece(diagonal_slot, part, index, diagonal_slot, to_partner, diagonal)
+
+    def far_diagonal(index):
+        wait_piece(far_diagonal_slot, 1, index, diagonal)
+        near(far_diagonal_slot, 1, diagonal, index=index)
+
+    for index in range(PIECES - 1):
+        hand_diagonal(0, index)
     wait_block(bridged_slot, 1, bridged)
     near(bridged_slot, 1, bridged)
-
-    wait_block(diagonal_slot, 0, diagonal)
-    send_block(diagonal_slot, 0, diagonal_slot, to_partner, diagonal)
+    hand_diagonal(1, 0)
+    near(diagonal_slot, 1, diagonal, index=0)
+    hand_diagonal(0, PIECES - 1)
     near(diagonal_slot, 0, diagonal)
-    wait_block(far_diagonal_slot, 0, diagonal)
+    hand_diagonal(1, 1)
+    near(diagonal_slot, 1, diagonal, index=1)
+    for index in range(PIECES):
+        wait_piece(far_diagonal_slot, 0, index, diagonal)
     near(far_diagonal_slot, 0, diagonal)
     for hop in range(3, levels):
         hand_crossed(hop)
-    for index in range(PIECES):
-        wait_piece(diagonal_slot, 1, index, diagonal)
-        send_piece(diagonal_slot, 1, index, diagonal_slot, to_partner, diagonal)
-        near(diagonal_slot, 1, diagonal, index=index)
-        if index > 0:
-            wait_piece(far_diagonal_slot, 1, index - 1, diagonal)
-            near(far_diagonal_slot, 1, diagonal, index=index - 1)
+    far_diagonal(0)
+    far_diagonal(1)
 
     for hop in range(1, levels):
         for step in (-hop, hop):
@@ -408,12 +446,14 @@
             wait_coeff(beside + 1 - 2 * core + 4 * step, crossed(step))
     theirs = fields.at[pl.ds(2 * other, 2)]
     receive(theirs, field_sem.at[4 + other])
+    far_load.wait()
     field = dot(nested[...], jnp.concatenate([fields[k] for k in range(4)], axis=1))
     for m in range(coupling.shape[0]):
         field = field + dot(coupling[m], coeffs[far_ref[0, 0, m]])
     field_ref[...] = field.astype(jnp.bfloat16)
-    wait_piece(far_diagonal_slot, 1, PIECES - 1, diagonal)
-    near(far_diagonal_slot, 1, diagonal, index=PIECES - 1)
+    hand_diagonal(1, 2)
+    near(diagonal_slot, 1, diagonal, index=2)
+    far_diagonal(2)
 
     for condition, copy in sent:
         if condition is None:
@@ -422,15 +462,22 @@
             pl.when(condition)(copy.wait_send)
 
 
-def finish_kernel(count_ref, acc_ref, field_ref, basis_ref, out_ref):
-    rows, vecs = out_ref.shape
-    half = vecs // 2
-    row = lax.broadcasted_iota(jnp.int32, (rows, half), 0) + pl.program_id(0) * rows
-    live = row < count_ref[0, 0]
-    for part in range(2):
-        columns = slice(part * half, (part + 1) * half)
-        value = acc_ref[part] + dot(basis_ref[0, 0], field_ref[:, columns])
-        out_ref[:, columns] = jnp.where(live, value, 0.0)
+def finish_kernel(count_ref, acc_ref, field_ref, basis_ref, out_ref, staged, sem):
+    steps, rows = staged.shape[:2]
+    half = acc_ref.shape[2]
+    copies = []
+    for step in range(steps):
+        span = slice(step * rows, (step + 1) * rows)
+        live = lax.broadcasted_iota(jnp.int32, (rows, half), 0) < count_ref[0, 0] - step * rows
+        for part in range(2):
+            columns = slice(part * half, (part + 1) * half)
+            value = acc_ref[part, span] + dot(basis_ref[0, 0, span], field_ref[:, columns])
+            staged[step, :, columns] = jnp.where(live, value, 0.0)
+        copy = pltpu.make_async_copy(staged.at[step], out_ref.at[span], sem.at[step])
+        copy.start()
+        copies.append(copy)
+    for copy in copies:
+        copy.wait()
 
 
 def body(
@@ -460,9 +507,11 @@
             jax.ShapeDtypeStruct((2, rows, half), jnp.float32),
             jax.ShapeDtypeStruct((rank, vecs), jnp.bfloat16),
         ),
-        in_specs=[smem] * 3 + [hbm] * 6,
+        in_specs=[smem] + [hbm] * 8,
         out_specs=(vmem, vmem),
         scratch_shapes=[
+            pltpu.SMEM(near_list.shape, jnp.int32),
+            pltpu.SMEM(far_list.shape, jnp.int32),
             pltpu.VMEM((rows, vecs), jnp.bfloat16),
             pltpu.VMEM(near_tiles.shape[2:], jnp.bfloat16),
             pltpu.VMEM(leaf_basis.shape[2:], jnp.bfloat16),
@@ -476,50 +525,51 @@
             pltpu.VMEM((2, rank, quarter), jnp.bfloat16),
             pltpu.VMEM((2, rank, quarter), jnp.float32),
             pltpu.VMEM((rank, quarter), jnp.bfloat16),
-            pltpu.VMEM((levels, rank, quarter), jnp.bfloat16),
+            pltpu.VMEM((2, rank, quarter), jnp.bfloat16),
+            pltpu.VMEM((2, rank, quarter), jnp.bfloat16),
             pltpu.VMEM((clusters, rank, quarter), jnp.bfloat16),
             pltpu.VMEM((4, rank, quarter), jnp.bfloat16),
             dma((near_tiles.shape[2],)),
-            dma((5,)),
+            dma((7,)),
             dma((send_count(levels, clusters),)),
             dma((SLOTS, 2)),
             dma((SLOTS, 2, PIECES)),
             dma((leaves,)),
             dma((1,)),
             dma((1,)),
-            dma((levels,)),
+            dma((2,)),
             dma((clusters,)),
             dma((6,)),
         ],
         compiler_params=pltpu.CompilerParams(
-            collective_id=0, has_side_effects=True, vmem_limit_bytes=62 * 1024 * 1024
+            collective_id=0, has_side_effects=True, vmem_limit_bytes=48 * 1024 * 1024
         ),
     )(
-        near_list,
-        far_list,
         row_counts,
-        vectors,
-        near_tiles,
-        leaf_basis,
-        transfer,
-        coupling,
-        top_coupling,
+        *[
+            pltpu.with_memory_space_constraint(array, pltpu.HBM)
+            for array in (
+                near_list,
+                far_list,
+                vectors,
+                near_tiles,
+                leaf_basis,
+                transfer,
+                coupling,
+                top_coupling,
+            )
+        ],
     )
-    steps = PIECES
     result = pl.pallas_call(
         finish_kernel,
         out_shape=jax.ShapeDtypeStruct((rows, vecs), jnp.float32),
-        grid=(steps,),
-        in_specs=[
-            smem,
-            pl.BlockSpec((2, rows // steps, half), lambda i: (0, i, 0)),
-            pl.BlockSpec((rank, vecs), lambda i: (0, 0)),
-            pl.BlockSpec((1, 1, rows // steps, rank), lambda i: (0, 0, i, 0)),
+        in_specs=[smem, vmem, vmem, vmem],
+        out_specs=pl.BlockSpec(memory_space=pl.ANY),
+        scratch_shapes=[
+            pltpu.VMEM((PIECES, rows // PIECES, vecs), jnp.float32),
+            dma((PIECES,)),
         ],
-        out_specs=pl.BlockSpec((rows // steps, vecs), lambda i: (i, 0)),
-        compiler_params=pltpu.CompilerParams(
-            dimension_semantics=("arbitrary",), vmem_limit_bytes=12 * 1024 * 1024
-        ),
+        compiler_params=pltpu.CompilerParams(vmem_limit_bytes=8 * 1024 * 1024),
     )(row_counts, acc, field, leaf_basis)
     return result[None, None]
 

time: 53.7 us -> 46.5 us (0.87)
  the two profiles are of different devices: /device:TPU:17 before, /device:TPU:5 now
where the time goes in v2:
time: 46.5 us; the launch traced here: 46.4 us
  Pallas kernels  45.7 us (98%)
  between operations  0.68 us (1%)
    pallas_call x1, Pallas kernels, body(): pl.pallas_call(functools.partial(exchange_kernel, levels, clusters), out_...  44.3 us
    pallas_call x1, Pallas kernels, body(): pl.pallas_call(finish_kernel, out_shape=jax.ShapeDtypeStruct((rows, vecs)...  1.38 us

profile of v2, /device:TPU:5, one launch (start us, length us, event | category | flops | bytes accessed | tf_op | source)
XLA Modules:
  0.0 46.4 jit_solution(5164214669857020780)
XLA Ops:
  0.7 0.0 copy-start
  0.7 44.3 %shard_map.91 = (f32[2,768,256]{2,1,0:T(8,128)S(1)}, bf16[128,512]{1,0:T(8,128)(2,1)S(1)}) custom-call(s32[1,1]{1,0:T(1,128)S(6)} %copy.10.count_ref, s32[1,1,8]{2,1,0:T(1,128)} %near_source.1, s32[1,1,7]{2,1,0:T(1,128)} %far_source.1, bf16[1,1,768,512]{3,2,1,0:T(8,128)(2,1)} %vectors_ref.1, bf16[1,1,8,768,768]{4,3,2,1,0:T(8,128)(2,1)} %tiles_ref.1, ...), custom_call_target="tpu_custom_call" | custom-call | tf_op jit(solution)/shard_map/pallas_call | solution.py:504
  45.0 0.0 copy-done
  45.0 1.4 %shard_map.92 = f32[768,512]{1,0:T(8,128)} custom-call(s32[1,1]{1,0:T(1,128)S(6)} %copy.10.count_ref, f32[2,768,256]{2,1,0:T(8,128)S(1)} %get-tuple-element.7.acc_ref, bf16[128,512]{1,0:T(8,128)(2,1)S(1)} %get-tuple-element.8.field_ref, bf16[1,1,768,128]{3,2,1,0:T(8,128)(2,1)S(1)} %copy-done), custom_call_target="tpu_custom_call" | custom-call | tf_op jit(solution)/shard_map/pallas_call | solution.py:563
Async XLA Ops:
  0.7 44.4 %copy-start = (bf16[1,1,768,128]{3,2,1,0:T(8,128)(2,1)S(1)}, bf16[1,1,768,128]{3,2,1,0:T(8,128)(2,1)}, u32[]{:S(2)}) copy-start(bf16[1,1,768,128]{3,2,1,0:T(8,128)(2,1)} %basis_ref.3) | copy-start | bytes 589828

commit v3 on v2

--- a/solution.py
+++ b/solution.py
@@ -37,7 +37,6 @@
     coupling_ref,
     top_ref,
     acc,
-    field_ref,
     near_ref,
     far_ref,
     raw,
@@ -50,7 +49,6 @@
     coeffs,
     halves,
     half_in,
-    quarters,
     partial,
     quarter_in,
     line_out,
@@ -80,18 +78,21 @@
     above = level < levels - 1
     below = level > 0
     first_column = column == 0
-    rows, vecs = raw.shape
-    half = vecs // 2
-    quarter = vecs // 4
+    rows, half = raw.shape[1:]
+    vecs = 2 * half
+    quarter = half // 2
     piece = rows // PIECES
     tile_count = tiles.shape[0]
 
     def load(source, target, sem):
         return pltpu.make_async_copy(source, target, sem)
 
-    raw_load = load(vectors_ref.at[0, 0], raw, load_sem.at[0])
-    basis_load = load(basis_ref.at[0, 0], basis, load_sem.at[1])
-    nested_load = load(nested_ref.at[0, 0], nested, load_sem.at[2])
+    raw_loads = [
+        load(vectors_ref.at[0, 0, :, pl.ds(part * half, half)], raw.at[part], load_sem.at[part])
+        for part in range(2)
+    ]
+    basis_load = load(basis_ref.at[0, 0], basis, load_sem.at[2])
+    nested_load = load(nested_ref.at[0, 0], nested, load_sem.at[7])
     coupling_load = load(coupling_ref.at[0, 0], coupling, load_sem.at[3])
     top_load = load(top_ref.at[0], top, load_sem.at[4])
     tile_loads = [load(tiles_ref.at[0, 0, k], tiles.at[k], tile_sem.at[k]) for k in range(tile_count)]
@@ -110,8 +111,7 @@
     pl.when(above)(lambda: greet({"leaf": me + 4}))
     pl.when(below)(lambda: greet({"leaf": me - 4}))
     expected = clusters + 1 + above.astype(jnp.int32) + below.astype(jnp.int32)
-    loads = [raw_load, basis_load, nested_load, near_load]
-    for copy in loads + tile_loads + [far_load, coupling_load, top_load]:
+    for copy in raw_loads + [basis_load, nested_load, near_load]:
         copy.start()
 
     sent = []
@@ -253,41 +253,46 @@
         else:
             pl.when(condition)(run)
 
-    raw_load.wait()
+    own_beside = own_slot + 4 * column - 2
+
+    def send_own(part, index):
+        send_piece(own_slot, part, index, core, to_above, above)
+        send_piece(own_slot, part, index, core + 8, to_below, below)
+
     live = lax.broadcasted_iota(jnp.int32, (rows, half), 0) < count_ref[0, 0]
+
+    def mask(part):
+        raw_loads[part].wait()
+        window[own_slot, part] = jnp.where(live, raw[part], jnp.zeros((), jnp.bfloat16))
+
+    mask(0)
+    pl.semaphore_wait(barrier, expected)
+    for index in range(PIECES - 1):
+        send_piece(own_slot, 0, index, own_beside, to_beside)
+    send_own(0, 0)
+    mask(1)
     basis_load.wait()
     for part in range(2):
-        columns = slice(part * half, (part + 1) * half)
-        masked = jnp.where(live, raw[:, columns], jnp.zeros((), jnp.bfloat16))
-        window[own_slot, part] = masked
-        coeffs[me, :, columns] = contract(basis[...], masked).astype(jnp.bfloat16)
+        product = contract(basis[...], window[own_slot, part])
+        coeffs[me, :, part * half : (part + 1) * half] = product.astype(jnp.bfloat16)
     nested_load.wait()
     for part in range(2):
         halves[part] = contract(nested[...], coeffs[me, :, part * half : (part + 1) * half])
-    pl.semaphore_wait(barrier, expected)
-
-    own_beside = own_slot + 4 * column - 2
     send_coeff(me, to_above, above)
     send_coeff(me, to_below, below)
+    for index in range(1, PIECES):
+        send_own(0, index)
     send(halves.at[other], half_in, half_sem.at[0], to_partner)
-    for index in range(PIECES - 1):
-        send_piece(own_slot, 0, index, own_beside, to_beside)
-    send_block(own_slot, 0, core, to_above, above)
-    send_block(own_slot, 0, core + 8, to_below, below)
     for part in range(2):
         send_block(own_slot, part, own_slot, to_partner)
-
-    def send_own(index):
-        send_piece(own_slot, 1, index, core, to_above, above)
-        send_piece(own_slot, 1, index, core + 8, to_below, below)
+    for copy in tile_loads + [far_load, coupling_load, top_load]:
+        copy.start()
 
     receive(half_in, half_sem.at[0])
     total = halves[core] + half_in[...]
     for part in range(2):
-        value = total[:, part * quarter : (part + 1) * quarter]
-        partial[part] = value
-        quarters[part] = value.astype(jnp.bfloat16)
-    send(quarters.at[1 - column], quarter_in, quarter_sem.at[0], to_beside)
+        partial[part] = total[:, part * quarter : (part + 1) * quarter]
+    send(partial.at[1 - column], quarter_in, quarter_sem.at[0], to_beside)
     send_piece(own_slot, 0, PIECES - 1, own_beside, to_beside)
     for copy in [near_load] + tile_loads:
         copy.wait()
@@ -301,7 +306,7 @@
     cross_coeffs(1)
     send_block(own_slot, 1, own_beside, to_beside)
     receive(quarter_in, quarter_sem.at[0])
-    partial[column] += quarter_in[...].astype(jnp.float32)
+    partial[column] += quarter_in[...]
 
     def line(turn):
         for way, at, step in ((0, turn - 1, 4), (1, levels - turn, -4)):
@@ -314,13 +319,13 @@
                 def _(way=way):
                     value = partial[column]
                     if turn > 1:
-                        value = value + line_in[way].astype(jnp.float32)
-                    line_out[way] = value.astype(jnp.bfloat16)
+                        value = value + line_in[way]
+                    line_out[way] = value
 
                 send(line_out.at[way], line_in.at[way], line_sem.at[way], {"leaf": me + step}, here)
 
     line(1)
-    send_own(0)
+    send_own(1, 0)
 
     bridged_slot = jnp.where(core == 0, 1, 8)
     bridged = jnp.logical_or(
@@ -343,13 +348,14 @@
         wait_piece(beside_slot, 0, index)
     send_block(beside_slot, 0, beside_slot, to_partner)
     near(beside_slot, 0)
-    wait_block(below_slot, 0, below)
-    wait_block(above_slot, 0, above)
+    for index in range(PIECES):
+        wait_piece(below_slot, 0, index, below)
+        wait_piece(above_slot, 0, index, above)
     hand_neighbours(0)
     near(below_slot, 0, below)
     near(above_slot, 0, above)
     line(2)
-    send_own(1)
+    send_own(1, 1)
 
     hand_crossed(1)
     if levels > 2:
@@ -363,7 +369,7 @@
     near(bridged_slot, 0, bridged)
     for turn in range(3, levels):
         line(turn)
-    send_own(2)
+    send_own(1, 2)
 
     wait_block(beside_slot, 1)
     for index in range(PIECES):
@@ -375,7 +381,7 @@
         line(levels)
     whole = partial[column]
     for way, condition in ((0, below), (1, above)):
-        whole = whole + jnp.where(condition, line_in[way].astype(jnp.float32), 0.0)
+        whole = whole + jnp.where(condition, line_in[way], 0.0)
     parents[cluster] = whole.astype(jnp.bfloat16)
     for step in range(1, clusters):
         send(
@@ -450,7 +456,9 @@
     field = dot(nested[...], jnp.concatenate([fields[k] for k in range(4)], axis=1))
     for m in range(coupling.shape[0]):
         field = field + dot(coupling[m], coeffs[far_ref[0, 0, m]])
-    field_ref[...] = field.astype(jnp.bfloat16)
+    field = field.astype(jnp.bfloat16)
+    for part in range(2):
+        acc[part] += dot(basis[...], field[:, part * half : (part + 1) * half])
     hand_diagonal(1, 2)
     near(diagonal_slot, 1, diagonal, index=2)
     far_diagonal(2)
@@ -462,7 +470,7 @@
             pl.when(condition)(copy.wait_send)
 
 
-def finish_kernel(count_ref, acc_ref, field_ref, basis_ref, out_ref, staged, sem):
+def finish_kernel(count_ref, acc_ref, out_ref, staged, sem):
     steps, rows = staged.shape[:2]
     half = acc_ref.shape[2]
     copies = []
@@ -471,8 +479,7 @@
         live = lax.broadcasted_iota(jnp.int32, (rows, half), 0) < count_ref[0, 0] - step * rows
         for part in range(2):
             columns = slice(part * half, (part + 1) * half)
-            value = acc_ref[part, span] + dot(basis_ref[0, 0, span], field_ref[:, columns])
-            staged[step, :, columns] = jnp.where(live, value, 0.0)
+            staged[step, :, columns] = jnp.where(live, acc_ref[part, span], 0.0)
         copy = pltpu.make_async_copy(staged.at[step], out_ref.at[span], sem.at[step])
         copy.start()
         copies.append(copy)
@@ -501,18 +508,15 @@
     vmem = pl.BlockSpec(memory_space=pltpu.VMEM)
     hbm = pl.BlockSpec(memory_space=pltpu.HBM)
     dma = pltpu.SemaphoreType.DMA
-    acc, field = pl.pallas_call(
+    acc = pl.pallas_call(
         functools.partial(exchange_kernel, levels, clusters),
-        out_shape=(
-            jax.ShapeDtypeStruct((2, rows, half), jnp.float32),
-            jax.ShapeDtypeStruct((rank, vecs), jnp.bfloat16),
-        ),
+        out_shape=jax.ShapeDtypeStruct((2, rows, half), jnp.float32),
         in_specs=[smem] + [hbm] * 8,
-        out_specs=(vmem, vmem),
+        out_specs=vmem,
         scratch_shapes=[
             pltpu.SMEM(near_list.shape, jnp.int32),
             pltpu.SMEM(far_list.shape, jnp.int32),
-            pltpu.VMEM((rows, vecs), jnp.bfloat16),
+            pltpu.VMEM((2, rows, half), jnp.bfloat16),
             pltpu.VMEM(near_tiles.shape[2:], jnp.bfloat16),
             pltpu.VMEM(leaf_basis.shape[2:], jnp.bfloat16),
             pltpu.VMEM(transfer.shape[2:], jnp.bfloat16),
@@ -522,15 +526,14 @@
             pltpu.VMEM((leaves, rank, vecs), jnp.bfloat16),
             pltpu.VMEM((2, rank, half), jnp.float32),
             pltpu.VMEM((rank, half), jnp.float32),
-            pltpu.VMEM((2, rank, quarter), jnp.bfloat16),
             pltpu.VMEM((2, rank, quarter), jnp.float32),
-            pltpu.VMEM((rank, quarter), jnp.bfloat16),
-            pltpu.VMEM((2, rank, quarter), jnp.bfloat16),
-            pltpu.VMEM((2, rank, quarter), jnp.bfloat16),
+            pltpu.VMEM((rank, quarter), jnp.float32),
+            pltpu.VMEM((2, rank, quarter), jnp.float32),
+            pltpu.VMEM((2, rank, quarter), jnp.float32),
             pltpu.VMEM((clusters, rank, quarter), jnp.bfloat16),
             pltpu.VMEM((4, rank, quarter), jnp.bfloat16),
             dma((near_tiles.shape[2],)),
-            dma((7,)),
+            dma((8,)),
             dma((send_count(levels, clusters),)),
             dma((SLOTS, 2)),
             dma((SLOTS, 2, PIECES)),
@@ -563,14 +566,14 @@
     result = pl.pallas_call(
         finish_kernel,
         out_shape=jax.ShapeDtypeStruct((rows, vecs), jnp.float32),
-        in_specs=[smem, vmem, vmem, vmem],
+        in_specs=[smem, vmem],
         out_specs=pl.BlockSpec(memory_space=pl.ANY),
         scratch_shapes=[
             pltpu.VMEM((PIECES, rows // PIECES, vecs), jnp.float32),
             dma((PIECES,)),
         ],
         compiler_params=pltpu.CompilerParams(vmem_limit_bytes=8 * 1024 * 1024),
-    )(row_counts, acc, field, leaf_basis)
+    )(row_counts, acc)
     return result[None, None]
 
 

time: 46.5 us -> 45.3 us (0.974)
  Pallas kernels: 45.7 us -> 44.5 us
    pallas_call x1, Pallas kernels: 44.3 us -> 43.2 us  [body(): pl.pallas_call(functools.partial(exchange_kernel, levels, clusters), out_...]
where the time goes in v3:
time: 45.3 us; the launch traced here: 45.1 us
  Pallas kernels  44.5 us (98%)
  between operations  0.66 us (1%)
    pallas_call x1, Pallas kernels, body(): pl.pallas_call(functools.partial(exchange_kernel, levels, clusters), out_...  43.2 us
    pallas_call x1, Pallas kernels, body(): pl.pallas_call(finish_kernel, out_shape=jax.ShapeDtypeStruct((rows, vecs)...  1.21 us

profile of v3, /device:TPU:5, one launch (start us, length us, event | category | flops | bytes accessed | tf_op | source)
XLA Modules:
  0.0 45.1 jit_solution(8745318879180344769)
XLA Ops:
  0.7 43.2 %shard_map.91.acc_ref = f32[2,768,256]{2,1,0:T(8,128)S(1)} custom-call(s32[1,1]{1,0:T(1,128)S(6)} %copy.10.count_ref, s32[1,1,8]{2,1,0:T(1,128)} %near_source.1, s32[1,1,7]{2,1,0:T(1,128)} %far_source.1, bf16[1,1,768,512]{3,2,1,0:T(8,128)(2,1)} %vectors_ref.1, bf16[1,1,8,768,768]{4,3,2,1,0:T(8,128)(2,1)} %tiles_ref.1, bf16[1,1,768,128]{3,2,1,0:T(8,128)(2,1)} %basis_ref.1, ...), custom_call_target="tpu_custom_call" | custom-call | tf_op jit(solution)/shard_map/pallas_call | solution.py:511
  43.9 1.2 %shard_map.92 = f32[768,512]{1,0:T(8,128)} custom-call(s32[1,1]{1,0:T(1,128)S(6)} %copy.10.count_ref, f32[2,768,256]{2,1,0:T(8,128)S(1)} %shard_map.91.acc_ref), custom_call_target="tpu_custom_call" | custom-call | tf_op jit(solution)/shard_map/pallas_call | solution.py:566

commit v4 on v3

--- a/solution.py
+++ b/solution.py
@@ -10,6 +10,32 @@
 REACH = 4
 SLOTS = 2 * REACH + 2
 PIECES = 3
+SPANS = ((0, 1), (1, 3), (3, 5), (5, 6))
+BESIDE, BELOW, ABOVE, PARTNER, FAR_BESIDE, BRIDGED, DIAGONAL, FAR_DIAGONAL = 0, 2, 4, 6, 8, 10, 12, 15
+SPAN, FAR_SPAN = 16, 16 + len(SPANS)
+ARRIVALS = FAR_SPAN + len(SPANS)
+(
+    TO_BESIDE,
+    TO_ABOVE,
+    TO_BELOW,
+    TO_PARTNER,
+    OVER,
+    OVER_SPAN,
+    ALONG,
+    HAND_BESIDE,
+    HAND_COLUMN,
+    HAND_DIAGONAL,
+    COEFF_ABOVE,
+    COEFF_BELOW,
+    COEFF_BESIDE,
+    COEFF_PARTNER,
+    HALF,
+    QUARTER,
+    LINE,
+    FIELD,
+    FIELD_PAIR,
+    PARENT,
+) = range(20)
 
 
 def contract(left, right):
@@ -18,10 +44,6 @@
 
 def dot(left, right):
     return jnp.dot(left, right, preferred_element_type=jnp.float32)
-
-
-def send_count(levels, clusters):
-    return 40 + 12 * levels + clusters
 
 
 def exchange_kernel(
@@ -55,11 +77,9 @@
     line_in,
     parents,
     fields,
-    tile_sem,
     load_sem,
     send_sem,
     block_sem,
-    piece_sem,
     coeff_sem,
     half_sem,
     quarter_sem,
@@ -81,6 +101,7 @@
     rows, half = raw.shape[1:]
     vecs = 2 * half
     quarter = half // 2
+    sixth = rows // 6
     piece = rows // PIECES
     tile_count = tiles.shape[0]
 
@@ -95,7 +116,8 @@
     nested_load = load(nested_ref.at[0, 0], nested, load_sem.at[7])
     coupling_load = load(coupling_ref.at[0, 0], coupling, load_sem.at[3])
     top_load = load(top_ref.at[0], top, load_sem.at[4])
-    tile_loads = [load(tiles_ref.at[0, 0, k], tiles.at[k], tile_sem.at[k]) for k in range(tile_count)]
+    tile_loads = [load(tiles_ref.at[0, 0, k], tiles.at[k], load_sem.at[8]) for k in range(tile_count)]
+    all_tiles = load(tiles_ref.at[0, 0], tiles, load_sem.at[8])
     near_load = load(near_source, near_ref, load_sem.at[5])
     far_load = load(far_source, far_ref, load_sem.at[6])
 
@@ -114,36 +136,36 @@
     for copy in raw_loads + [basis_load, nested_load, near_load]:
         copy.start()
 
-    sent = []
-
-    def send(source, target, sem, peer, condition=None):
-        copy = pltpu.make_async_remote_copy(
+    def remote(source, target, sem, peer, done):
+        return pltpu.make_async_remote_copy(
             src_ref=source,
             dst_ref=target,
-            send_sem=send_sem.at[len(sent)],
+            send_sem=send_sem.at[done],
             recv_sem=sem,
             device_id=peer,
             device_id_type=pl.DeviceIdType.MESH,
         )
-        sent.append((condition, copy))
+
+    def send(source, target, sem, peer, done, condition=None):
+        copy = remote(source, target, sem, peer, done)
         if condition is None:
             copy.start()
         else:
             pl.when(condition)(copy.start)
 
     def receive(block, sem, condition=None):
-        copy = pltpu.make_async_remote_copy(
-            src_ref=block,
-            dst_ref=block,
-            send_sem=send_sem.at[0],
-            recv_sem=sem,
-            device_id={"leaf": partner},
-            device_id_type=pl.DeviceIdType.MESH,
-        )
+        copy = remote(block, block, sem, {"leaf": partner}, 0)
         if condition is None:
             copy.wait_recv()
         else:
             pl.when(condition)(copy.wait_recv)
+
+    def drain(block, done, condition=None):
+        copy = remote(block, block, block_sem.at[0], {"leaf": partner}, done)
+        if condition is None:
+            copy.wait_send()
+        else:
+            pl.when(condition)(copy.wait_send)
 
     to_partner, to_beside = {"leaf": partner}, {"leaf": beside}
     to_above, to_below = {"leaf": me + 4}, {"leaf": me - 4}
@@ -163,32 +185,61 @@
     relay_up = jnp.logical_and(first_column, above)
     relay_down = jnp.logical_and(column == 1, below)
 
-    def send_block(slot, part, target, peer, condition=None):
-        send(window.at[slot, part], window.at[target, part], block_sem.at[target, part], peer, condition)
-
-    def wait_block(slot, part, condition=None):
-        receive(window.at[slot, part], block_sem.at[slot, part], condition)
-
-    def span_of(index):
-        return pl.ds(index * piece, piece)
-
-    def send_piece(slot, part, index, target, peer, condition=None):
+    def send_block(slot, part, target, arrival, peer, done, condition=None):
         send(
-            window.at[slot, part, span_of(index)],
-            window.at[target, part, span_of(index)],
-            piece_sem.at[target, part, index],
+            window.at[slot, part],
+            window.at[target, part],
+            block_sem.at[arrival + part],
             peer,
+            done,
             condition,
         )
 
-    def wait_piece(slot, part, index, condition=None):
-        receive(window.at[slot, part, span_of(index)], piece_sem.at[slot, part, index], condition)
-
-    def send_coeff(leaf, peer, condition=None):
-        send(coeffs.at[leaf], coeffs.at[leaf], coeff_sem.at[leaf], peer, condition)
+    def wait_block(slot, part, arrival, condition=None):
+        receive(window.at[slot, part], block_sem.at[arrival + part], condition)
+
+    def rows_of(index):
+        return pl.ds(index * piece, piece)
+
+    def span_of(index):
+        start, stop = SPANS[index]
+        return pl.ds(start * sixth, (stop - start) * sixth)
+
+    def send_rows(slot, part, span, target, arrival, peer, done, condition=None):
+        send(
+            window.at[slot, part, span],
+            window.at[target, part, span],
+            block_sem.at[arrival],
+            peer,
+            done,
+            condition,
+        )
+
+    def wait_rows(slot, part, span, arrival, condition=None):
+        receive(window.at[slot, part, span], block_sem.at[arrival], condition)
+
+    def send_coeff(leaf, peer, done, condition=None):
+        send(coeffs.at[leaf], coeffs.at[leaf], coeff_sem.at[lax.div(leaf, 2)], peer, done, condition)
+
+    def hand_coeff(leaf, condition):
+        send(
+            coeffs.at[leaf],
+            coeffs.at[leaf],
+            coeff_sem.at[2 * levels],
+            to_partner,
+            COEFF_PARTNER,
+            condition,
+        )
 
     def wait_coeff(leaf, condition=None):
-        receive(coeffs.at[leaf], coeff_sem.at[leaf], condition)
+        receive(coeffs.at[leaf], coeff_sem.at[lax.div(leaf, 2)], condition)
+
+    def for_count(conditions, run):
+        count = 0
+        for condition in conditions:
+            count = count + jnp.where(condition, 1, 0)
+        for n in range(1, len(conditions) + 1):
+            pl.when(count == n)(lambda n=n: run(coeffs.at[pl.ds(0, n)]))
 
     def exists(step):
         return jnp.logical_and(level + step >= 0, level + step < levels)
@@ -215,18 +266,18 @@
         for step in (-hop, hop):
             wait_coeff(me + 4 * step, exists(step))
         if hop + 1 < levels:
-            send_coeff(me - 4 * hop, to_above, jnp.logical_and(exists(-hop), above))
-            send_coeff(me + 4 * hop, to_below, jnp.logical_and(exists(hop), below))
+            send_coeff(me - 4 * hop, to_above, COEFF_ABOVE, jnp.logical_and(exists(-hop), above))
+            send_coeff(me + 4 * hop, to_below, COEFF_BELOW, jnp.logical_and(exists(hop), below))
 
     def cross_coeffs(hop):
         for step in (-hop, hop):
-            send_coeff(me + 4 * step, to_beside, crossing(step))
-            send_coeff(me + 4 * step, to_partner, handed(step, core))
+            send_coeff(me + 4 * step, to_beside, COEFF_BESIDE, crossing(step))
+            hand_coeff(me + 4 * step, handed(step, core))
 
     def hand_crossed(hop):
         for step in (-hop, hop):
             wait_coeff(beside + 4 * step, crossed(step))
-            send_coeff(beside + 4 * step, to_partner, crossed(step))
+            hand_coeff(beside + 4 * step, crossed(step))
 
     def near(slot, part, condition=None, first=False, index=None):
         offset = slot - REACH - core
@@ -241,7 +292,8 @@
             if index is None:
                 product = dot(tiles[place], window[slot, part]) * scale
             else:
-                span = slice(index * piece, (index + 1) * piece)
+                start, stop = SPANS[index]
+                span = slice(start * sixth, stop * sixth)
                 product = dot(tiles[place, :, span], window[slot, part, span, :]) * scale
             if first:
                 acc[part] = product
@@ -256,8 +308,12 @@
     own_beside = own_slot + 4 * column - 2
 
     def send_own(part, index):
-        send_piece(own_slot, part, index, core, to_above, above)
-        send_piece(own_slot, part, index, core + 8, to_below, below)
+        span = rows_of(index)
+        send_rows(own_slot, part, span, core, BELOW + part, to_above, TO_ABOVE, above)
+        send_rows(own_slot, part, span, core + 8, ABOVE + part, to_below, TO_BELOW, below)
+
+    def send_first(index):
+        send_rows(own_slot, 0, rows_of(index), own_beside, BESIDE, to_beside, TO_BESIDE)
 
     live = lax.broadcasted_iota(jnp.int32, (rows, half), 0) < count_ref[0, 0]
 
@@ -268,7 +324,7 @@
     mask(0)
     pl.semaphore_wait(barrier, expected)
     for index in range(PIECES - 1):
-        send_piece(own_slot, 0, index, own_beside, to_beside)
+        send_first(index)
     send_own(0, 0)
     mask(1)
     basis_load.wait()
@@ -278,13 +334,13 @@
     nested_load.wait()
     for part in range(2):
         halves[part] = contract(nested[...], coeffs[me, :, part * half : (part + 1) * half])
-    send_coeff(me, to_above, above)
-    send_coeff(me, to_below, below)
+    send_coeff(me, to_above, COEFF_ABOVE, above)
+    send_coeff(me, to_below, COEFF_BELOW, below)
     for index in range(1, PIECES):
         send_own(0, index)
-    send(halves.at[other], half_in, half_sem.at[0], to_partner)
+    send(halves.at[other], half_in, half_sem.at[0], to_partner, HALF)
     for part in range(2):
-        send_block(own_slot, part, own_slot, to_partner)
+        send_block(own_slot, part, own_slot, PARTNER, to_partner, TO_PARTNER)
     for copy in tile_loads + [far_load, coupling_load, top_load]:
         copy.start()
 
@@ -292,19 +348,19 @@
     total = halves[core] + half_in[...]
     for part in range(2):
         partial[part] = total[:, part * quarter : (part + 1) * quarter]
-    send(partial.at[1 - column], quarter_in, quarter_sem.at[0], to_beside)
-    send_piece(own_slot, 0, PIECES - 1, own_beside, to_beside)
-    for copy in [near_load] + tile_loads:
-        copy.wait()
+    send(partial.at[1 - column], quarter_in, quarter_sem.at[0], to_beside, QUARTER)
+    send_first(PIECES - 1)
+    near_load.wait()
+    all_tiles.wait()
     near(own_slot, 0, first=True)
     near(own_slot, 1, first=True)
     for part in range(2):
-        wait_block(partner_slot, part)
+        wait_block(partner_slot, part, PARTNER)
         near(partner_slot, part)
 
     relay_coeffs(1)
     cross_coeffs(1)
-    send_block(own_slot, 1, own_beside, to_beside)
+    send_block(own_slot, 1, own_beside, BESIDE, to_beside, TO_BESIDE)
     receive(quarter_in, quarter_sem.at[0])
     partial[column] += quarter_in[...]
 
@@ -322,7 +378,7 @@
                         value = value + line_in[way]
                     line_out[way] = value
 
-                send(line_out.at[way], line_in.at[way], line_sem.at[way], {"leaf": me + step}, here)
+                send(line_out.at[way], line_in.at[way], line_sem.at[way], {"leaf": me + step}, LINE, here)
 
     line(1)
     send_own(1, 0)
@@ -337,20 +393,20 @@
     far_diagonal_slot = other + 2 + 4 * column
 
     def hand_neighbours(part):
-        send_block(below_slot, part, below_slot, to_partner, hand_below)
-        send_block(above_slot, part, above_slot, to_partner, hand_above)
+        send_block(below_slot, part, below_slot, BRIDGED, to_partner, HAND_COLUMN, hand_below)
+        send_block(above_slot, part, above_slot, BRIDGED, to_partner, HAND_COLUMN, hand_above)
 
     def send_over(index):
-        send_piece(below_slot, 0, index, core + 2, to_beside, relay_down)
-        send_piece(above_slot, 0, index, core + 6, to_beside, relay_up)
-
-    for index in range(PIECES):
-        wait_piece(beside_slot, 0, index)
-    send_block(beside_slot, 0, beside_slot, to_partner)
+        span = rows_of(index)
+        arrival = DIAGONAL + index
+        send_rows(below_slot, 0, span, core + 2, arrival, to_beside, OVER, relay_down)
+        send_rows(above_slot, 0, span, core + 6, arrival, to_beside, OVER, relay_up)
+
+    wait_block(beside_slot, 0, BESIDE)
+    send_block(beside_slot, 0, beside_slot, FAR_BESIDE, to_partner, HAND_BESIDE)
     near(beside_slot, 0)
-    for index in range(PIECES):
-        wait_piece(below_slot, 0, index, below)
-        wait_piece(above_slot, 0, index, above)
+    wait_block(below_slot, 0, BELOW, below)
+    wait_block(above_slot, 0, ABOVE, above)
     hand_neighbours(0)
     near(below_slot, 0, below)
     near(above_slot, 0, above)
@@ -361,21 +417,23 @@
     if levels > 2:
         relay_coeffs(2)
         cross_coeffs(2)
-    send_over(0)
-    send_over(1)
-    wait_block(far_beside_slot, 0)
+    for index in range(PIECES):
+        send_over(index)
+    wait_block(far_beside_slot, 0, FAR_BESIDE)
     near(far_beside_slot, 0)
-    wait_block(bridged_slot, 0, bridged)
+    wait_block(bridged_slot, 0, BRIDGED, bridged)
     near(bridged_slot, 0, bridged)
     for turn in range(3, levels):
         line(turn)
     send_own(1, 2)
 
-    wait_block(beside_slot, 1)
-    for index in range(PIECES):
-        send_piece(beside_slot, 1, index, core + 2, to_above, relay_up)
-        send_piece(beside_slot, 1, index, core + 6, to_below, relay_down)
-    send_block(beside_slot, 1, beside_slot, to_partner)
+    wait_block(beside_slot, 1, BESIDE)
+    for index in range(1, len(SPANS)):
+        span = span_of(index)
+        arrival = SPAN + index
+        send_rows(beside_slot, 1, span, core + 2, arrival, to_above, ALONG, relay_up)
+        send_rows(beside_slot, 1, span, core + 6, arrival, to_below, ALONG, relay_down)
+    send_block(beside_slot, 1, beside_slot, FAR_BESIDE, to_partner, HAND_BESIDE)
     near(beside_slot, 1)
     if levels > 2:
         line(levels)
@@ -389,8 +447,9 @@
             parents.at[cluster],
             parent_sem.at[cluster],
             {"top": lax.rem(cluster + step, clusters)},
+            PARENT + step - 1,
         )
-    wait_block(far_beside_slot, 1)
+    wait_block(far_beside_slot, 1, FAR_BESIDE)
     near(far_beside_slot, 1)
     coupling_load.wait()
     top_load.wait()
@@ -402,56 +461,70 @@
         over = over + dot(top[m], parents[lax.rem(cluster + 1 + m, clusters)])
     place = 2 * core + column
     fields[place] = over.astype(jnp.bfloat16)
-    send(fields.at[place], fields.at[place], field_sem.at[place], to_beside)
-    send_over(2)
+    send(fields.at[place], fields.at[place], field_sem.at[0], to_beside, FIELD)
     if levels > 2:
         hand_crossed(2)
     for hop in range(3, levels):
         relay_coeffs(hop)
         cross_coeffs(hop)
-    for index in range(PIECES):
-        wait_piece(below_slot, 1, index, below)
-        wait_piece(above_slot, 1, index, above)
+    wait_block(below_slot, 1, BELOW, below)
+    wait_block(above_slot, 1, ABOVE, above)
+    span = span_of(0)
+    send_rows(below_slot, 1, span, core + 2, SPAN, to_beside, OVER_SPAN, relay_down)
+    send_rows(above_slot, 1, span, core + 6, SPAN, to_beside, OVER_SPAN, relay_up)
     hand_neighbours(1)
     near(below_slot, 1, below)
     near(above_slot, 1, above)
+
+    def hand_first(index):
+        span = rows_of(index)
+        wait_rows(diagonal_slot, 0, span, DIAGONAL + index, diagonal)
+        send_rows(
+            diagonal_slot, 0, span, diagonal_slot, FAR_DIAGONAL, to_partner, HAND_DIAGONAL, diagonal
+        )
+
+    def hand_second(index):
+        span = span_of(index)
+        wait_rows(diagonal_slot, 1, span, SPAN + index, diagonal)
+        arrival = FAR_SPAN + index
+        send_rows(
+            diagonal_slot, 1, span, diagonal_slot, arrival, to_partner, HAND_DIAGONAL, diagonal
+        )
+
+    def far_second(index):
+        wait_rows(far_diagonal_slot, 1, span_of(index), FAR_SPAN + index, diagonal)
+        near(far_diagonal_slot, 1, diagonal, index=index)
+
+    def own_second(index):
+        near(diagonal_slot, 1, diagonal, index=index)
+
+    hand_first(0)
+    wait_block(bridged_slot, 1, BRIDGED, bridged)
+    near(bridged_slot, 1, bridged)
+    hand_second(1)
+    hand_first(1)
+    own_second(1)
+    hand_first(2)
+    hand_second(2)
+    near(diagonal_slot, 0, diagonal)
+    own_second(2)
     next_place = 2 * core + 1 - column
-    receive(fields.at[next_place], field_sem.at[next_place])
+    receive(fields.at[next_place], field_sem.at[0])
     pair = fields.at[pl.ds(2 * core, 2)]
-    send(pair, pair, field_sem.at[4 + core], to_partner)
-
-    def hand_diagonal(part, index):
-        wait_piece(diagonal_slot, part, index, diagonal)
-        send_piece(diagonal_slot, part, index, diagonal_slot, to_partner, diagonal)
-
-    def far_diagonal(index):
-        wait_piece(far_diagonal_slot, 1, index, diagonal)
-        near(far_diagonal_slot, 1, diagonal, index=index)
-
-    for index in range(PIECES - 1):
-        hand_diagonal(0, index)
-    wait_block(bridged_slot, 1, bridged)
-    near(bridged_slot, 1, bridged)
-    hand_diagonal(1, 0)
-    near(diagonal_slot, 1, diagonal, index=0)
-    hand_diagonal(0, PIECES - 1)
-    near(diagonal_slot, 0, diagonal)
-    hand_diagonal(1, 1)
-    near(diagonal_slot, 1, diagonal, index=1)
-    for index in range(PIECES):
-        wait_piece(far_diagonal_slot, 0, index, diagonal)
+    send(pair, pair, field_sem.at[1], to_partner, FIELD_PAIR)
+    wait_block(far_diagonal_slot, 0, FAR_DIAGONAL, diagonal)
     near(far_diagonal_slot, 0, diagonal)
+    far_second(1)
     for hop in range(3, levels):
         hand_crossed(hop)
-    far_diagonal(0)
-    far_diagonal(1)
-
-    for hop in range(1, levels):
-        for step in (-hop, hop):
-            wait_coeff(partner + 4 * step, handed(step, other))
-            wait_coeff(beside + 1 - 2 * core + 4 * step, crossed(step))
+    far_second(2)
+    hand_second(3)
+
+    steps = [step for hop in range(1, levels) for step in (-hop, hop)]
+    theirs_count = [handed(step, other) for step in steps] + [crossed(step) for step in steps]
+    for_count(theirs_count, lambda block: receive(block, coeff_sem.at[2 * levels]))
     theirs = fields.at[pl.ds(2 * other, 2)]
-    receive(theirs, field_sem.at[4 + other])
+    receive(theirs, field_sem.at[1])
     far_load.wait()
     field = dot(nested[...], jnp.concatenate([fields[k] for k in range(4)], axis=1))
     for m in range(coupling.shape[0]):
@@ -459,15 +532,41 @@
     field = field.astype(jnp.bfloat16)
     for part in range(2):
         acc[part] += dot(basis[...], field[:, part * half : (part + 1) * half])
-    hand_diagonal(1, 2)
-    near(diagonal_slot, 1, diagonal, index=2)
-    far_diagonal(2)
-
-    for condition, copy in sent:
-        if condition is None:
-            copy.wait_send()
-        else:
-            pl.when(condition)(copy.wait_send)
+    hand_second(0)
+    own_second(3)
+    own_second(0)
+    far_second(3)
+    far_second(0)
+
+    whole_block = window.at[own_slot]
+    for done, condition in (
+        (TO_BESIDE, None),
+        (TO_ABOVE, above),
+        (TO_BELOW, below),
+        (TO_PARTNER, None),
+        (HAND_BESIDE, None),
+        (HAND_COLUMN, jnp.logical_or(hand_below, hand_above)),
+        (HAND_DIAGONAL, diagonal),
+    ):
+        drain(whole_block, done, condition)
+    drain(window.at[own_slot, 0], OVER, relay_over)
+    drain(window.at[own_slot, 1, span_of(0)], OVER_SPAN, relay_over)
+    drain(window.at[own_slot, 1, pl.ds(sixth, 5 * sixth)], ALONG, relay_over)
+    drain(halves.at[0], HALF)
+    drain(partial.at[0], QUARTER)
+    drain(fields.at[0], FIELD)
+    drain(fields.at[pl.ds(0, 2)], FIELD_PAIR)
+    for step in range(1, clusters):
+        drain(parents.at[0], PARENT + step - 1)
+    drain(line_out.at[0], LINE, jnp.logical_xor(above, below))
+    drain(line_out, LINE, jnp.logical_and(above, below))
+    ours = [handed(step, core) for step in steps] + [crossed(step) for step in steps]
+    for_count(ours, lambda block: drain(block, COEFF_PARTNER))
+    for_count([crossing(step) for step in steps], lambda block: drain(block, COEFF_BESIDE))
+    up = [above] + [jnp.logical_and(exists(-hop), above) for hop in range(1, levels)]
+    down = [below] + [jnp.logical_and(exists(hop), below) for hop in range(1, levels)]
+    for_count(up, lambda block: drain(block, COEFF_ABOVE))
+    for_count(down, lambda block: drain(block, COEFF_BELOW))
 
 
 def finish_kernel(count_ref, acc_ref, out_ref, staged, sem):
@@ -532,17 +631,15 @@
             pltpu.VMEM((2, rank, quarter), jnp.float32),
             pltpu.VMEM((clusters, rank, quarter), jnp.bfloat16),
             pltpu.VMEM((4, rank, quarter), jnp.bfloat16),
-            dma((near_tiles.shape[2],)),
-            dma((8,)),
-            dma((send_count(levels, clusters),)),
-            dma((SLOTS, 2)),
-            dma((SLOTS, 2, PIECES)),
-            dma((leaves,)),
+            dma((9,)),
+            dma((PARENT + clusters - 1,)),
+            dma((ARRIVALS,)),
+            dma((leaves // 2 + 1,)),
             dma((1,)),
             dma((1,)),
             dma((2,)),
             dma((clusters,)),
-            dma((6,)),
+            dma((2,)),
         ],
         compiler_params=pltpu.CompilerParams(
             collective_id=0, has_side_effects=True, vmem_limit_bytes=48 * 1024 * 1024

time: 45.3 us -> 44.2 us (0.976)
  Pallas kernels: 44.5 us -> 43.4 us
    pallas_call x1, Pallas kernels: 43.2 us -> 42.2 us  [body(): pl.pallas_call(functools.partial(exchange_kernel, levels, clusters), out_...]
where the time goes in v4:
time: 44.2 us; the launch traced here: 44.1 us
  Pallas kernels  43.4 us (98%)
  between operations  0.66 us (1%)
    pallas_call x1, Pallas kernels, body(): pl.pallas_call(functools.partial(exchange_kernel, levels, clusters), out_...  42.2 us
    pallas_call x1, Pallas kernels, body(): pl.pallas_call(finish_kernel, out_shape=jax.ShapeDtypeStruct((rows, vecs)...  1.21 us

profile of v4, /device:TPU:5, one launch (start us, length us, event | category | flops | bytes accessed | tf_op | source)
XLA Modules:
  0.0 44.1 jit_solution(10299323755763681127)
XLA Ops:
  0.7 42.2 %shard_map.91.acc_ref = f32[2,768,256]{2,1,0:T(8,128)S(1)} custom-call(s32[1,1]{1,0:T(1,128)S(6)} %copy.10.count_ref, s32[1,1,8]{2,1,0:T(1,128)} %near_source.1, s32[1,1,7]{2,1,0:T(1,128)} %far_source.1, bf16[1,1,768,512]{3,2,1,0:T(8,128)(2,1)} %vectors_ref.1, bf16[1,1,8,768,768]{4,3,2,1,0:T(8,128)(2,1)} %tiles_ref.1, bf16[1,1,768,128]{3,2,1,0:T(8,128)(2,1)} %basis_ref.1, ...), custom_call_target="tpu_custom_call" | custom-call | tf_op jit(solution)/shard_map/pallas_call | solution.py:610
  42.8 1.2 %shard_map.92 = f32[768,512]{1,0:T(8,128)} custom-call(s32[1,1]{1,0:T(1,128)S(6)} %copy.10.count_ref, f32[2,768,256]{2,1,0:T(8,128)S(1)} %shard_map.91.acc_ref), custom_call_target="tpu_custom_call" | custom-call | tf_op jit(solution)/shard_map/pallas_call | solution.py:663

commit v5 on v4

--- a/solution.py
+++ b/solution.py
@@ -11,8 +11,9 @@
 SLOTS = 2 * REACH + 2
 PIECES = 3
 SPANS = ((0, 1), (1, 3), (3, 5), (5, 6))
-BESIDE, BELOW, ABOVE, PARTNER, FAR_BESIDE, BRIDGED, DIAGONAL, FAR_DIAGONAL = 0, 2, 4, 6, 8, 10, 12, 15
-SPAN, FAR_SPAN = 16, 16 + len(SPANS)
+BESIDE, BELOW, ABOVE, PARTNER, FAR_BESIDE, BRIDGED = 0, 2, 4, 6, 8, 10
+DIAGONAL, FAR_DIAGONAL, SPAN = 12, 12 + PIECES, 12 + 2 * PIECES
+FAR_SPAN = SPAN + len(SPANS)
 ARRIVALS = FAR_SPAN + len(SPANS)
 (
     TO_BESIDE,
@@ -279,7 +280,7 @@
             wait_coeff(beside + 4 * step, crossed(step))
             hand_coeff(beside + 4 * step, crossed(step))
 
-    def near(slot, part, condition=None, first=False, index=None):
+    def near(slot, part, condition=None, first=False, spans=None):
         offset = slot - REACH - core
         place, hit = 0, 0
         for k in range(tile_count):
@@ -289,12 +290,14 @@
         scale = hit.astype(jnp.float32)
 
         def run():
-            if index is None:
+            if spans is None:
                 product = dot(tiles[place], window[slot, part]) * scale
             else:
-                start, stop = SPANS[index]
-                span = slice(start * sixth, stop * sixth)
-                product = dot(tiles[place, :, span], window[slot, part, span, :]) * scale
+                product = 0.0
+                for start, stop in spans:
+                    span = slice(start * sixth, stop * sixth)
+                    product = product + dot(tiles[place, :, span], window[slot, part, span, :])
+                product = product * scale
             if first:
                 acc[part] = product
             else:
@@ -417,7 +420,7 @@
     if levels > 2:
         relay_coeffs(2)
         cross_coeffs(2)
-    for index in range(PIECES):
+    for index in range(PIECES - 1):
         send_over(index)
     wait_block(far_beside_slot, 0, FAR_BESIDE)
     near(far_beside_slot, 0)
@@ -428,13 +431,19 @@
     send_own(1, 2)
 
     wait_block(beside_slot, 1, BESIDE)
-    for index in range(1, len(SPANS)):
+    inner_up = jnp.logical_and(relay_up, level < levels - 2)
+    inner_down = jnp.logical_and(relay_down, level > 1)
+    for index in range(len(SPANS)):
         span = span_of(index)
         arrival = SPAN + index
-        send_rows(beside_slot, 1, span, core + 2, arrival, to_above, ALONG, relay_up)
-        send_rows(beside_slot, 1, span, core + 6, arrival, to_below, ALONG, relay_down)
+        up, down = (relay_up, relay_down) if index else (inner_up, inner_down)
+        send_rows(beside_slot, 1, span, core + 2, arrival, to_above, ALONG, up)
+        send_rows(beside_slot, 1, span, core + 6, arrival, to_below, ALONG, down)
     send_block(beside_slot, 1, beside_slot, FAR_BESIDE, to_partner, HAND_BESIDE)
     near(beside_slot, 1)
+    for hop in range(3, levels):
+        relay_coeffs(hop)
+        cross_coeffs(hop)
     if levels > 2:
         line(levels)
     whole = partial[column]
@@ -462,63 +471,66 @@
     place = 2 * core + column
     fields[place] = over.astype(jnp.bfloat16)
     send(fields.at[place], fields.at[place], field_sem.at[0], to_beside, FIELD)
+    send_over(PIECES - 1)
     if levels > 2:
         hand_crossed(2)
-    for hop in range(3, levels):
-        relay_coeffs(hop)
-        cross_coeffs(hop)
     wait_block(below_slot, 1, BELOW, below)
     wait_block(above_slot, 1, ABOVE, above)
     span = span_of(0)
-    send_rows(below_slot, 1, span, core + 2, SPAN, to_beside, OVER_SPAN, relay_down)
-    send_rows(above_slot, 1, span, core + 6, SPAN, to_beside, OVER_SPAN, relay_up)
+    last_down = jnp.logical_and(relay_down, level == levels - 1)
+    last_up = jnp.logical_and(relay_up, level == 0)
+    send_rows(below_slot, 1, span, core + 2, SPAN, to_beside, OVER_SPAN, last_down)
+    send_rows(above_slot, 1, span, core + 6, SPAN, to_beside, OVER_SPAN, last_up)
     hand_neighbours(1)
     near(below_slot, 1, below)
     near(above_slot, 1, above)
 
     def hand_first(index):
         span = rows_of(index)
+        arrival = FAR_DIAGONAL + index
         wait_rows(diagonal_slot, 0, span, DIAGONAL + index, diagonal)
-        send_rows(
-            diagonal_slot, 0, span, diagonal_slot, FAR_DIAGONAL, to_partner, HAND_DIAGONAL, diagonal
-        )
+        send_rows(diagonal_slot, 0, span, diagonal_slot, arrival, to_partner, HAND_DIAGONAL, diagonal)
+
+    def own_first(index):
+        near(diagonal_slot, 0, diagonal, spans=((2 * index, 2 * index + 2),))
+
+    def far_first(index):
+        wait_rows(far_diagonal_slot, 0, rows_of(index), FAR_DIAGONAL + index, diagonal)
+        near(far_diagonal_slot, 0, diagonal, spans=((2 * index, 2 * index + 2),))
 
     def hand_second(index):
         span = span_of(index)
+        arrival = FAR_SPAN + index
         wait_rows(diagonal_slot, 1, span, SPAN + index, diagonal)
-        arrival = FAR_SPAN + index
-        send_rows(
-            diagonal_slot, 1, span, diagonal_slot, arrival, to_partner, HAND_DIAGONAL, diagonal
-        )
-
-    def far_second(index):
-        wait_rows(far_diagonal_slot, 1, span_of(index), FAR_SPAN + index, diagonal)
-        near(far_diagonal_slot, 1, diagonal, index=index)
-
-    def own_second(index):
-        near(diagonal_slot, 1, diagonal, index=index)
+        send_rows(diagonal_slot, 1, span, diagonal_slot, arrival, to_partner, HAND_DIAGONAL, diagonal)
+
+    def own_second(*indices):
+        near(diagonal_slot, 1, diagonal, spans=[SPANS[index] for index in indices])
+
+    def far_second(*indices):
+        for index in indices:
+            wait_rows(far_diagonal_slot, 1, span_of(index), FAR_SPAN + index, diagonal)
+        near(far_diagonal_slot, 1, diagonal, spans=[SPANS[index] for index in indices])
 
     hand_first(0)
+    own_first(0)
     wait_block(bridged_slot, 1, BRIDGED, bridged)
     near(bridged_slot, 1, bridged)
     hand_second(1)
+    own_second(1)
     hand_first(1)
-    own_second(1)
-    hand_first(2)
-    hand_second(2)
-    near(diagonal_slot, 0, diagonal)
-    own_second(2)
+    own_first(1)
+    far_first(0)
+    far_second(1)
     next_place = 2 * core + 1 - column
     receive(fields.at[next_place], field_sem.at[0])
     pair = fields.at[pl.ds(2 * core, 2)]
     send(pair, pair, field_sem.at[1], to_partner, FIELD_PAIR)
-    wait_block(far_diagonal_slot, 0, FAR_DIAGONAL, diagonal)
-    near(far_diagonal_slot, 0, diagonal)
-    far_second(1)
     for hop in range(3, levels):
         hand_crossed(hop)
-    far_second(2)
-    hand_second(3)
+    far_first(1)
+    hand_second(2)
+    own_second(2)
 
     steps = [step for hop in range(1, levels) for step in (-hop, hop)]
     theirs_count = [handed(step, other) for step in steps] + [crossed(step) for step in steps]
@@ -532,11 +544,15 @@
     field = field.astype(jnp.bfloat16)
     for part in range(2):
         acc[part] += dot(basis[...], field[:, part * half : (part + 1) * half])
+
+    hand_first(2)
+    own_first(2)
+    hand_second(3)
+    far_second(2)
     hand_second(0)
-    own_second(3)
-    own_second(0)
-    far_second(3)
-    far_second(0)
+    own_second(3, 0)
+    far_first(2)
+    far_second(3, 0)
 
     whole_block = window.at[own_slot]
     for done, condition in (
@@ -550,8 +566,11 @@
     ):
         drain(whole_block, done, condition)
     drain(window.at[own_slot, 0], OVER, relay_over)
-    drain(window.at[own_slot, 1, span_of(0)], OVER_SPAN, relay_over)
-    drain(window.at[own_slot, 1, pl.ds(sixth, 5 * sixth)], ALONG, relay_over)
+    drain(window.at[own_slot, 1, span_of(0)], OVER_SPAN, jnp.logical_or(last_down, last_up))
+    inner = jnp.logical_or(inner_up, inner_down)
+    outer = jnp.logical_and(relay_over, jnp.logical_not(inner))
+    drain(window.at[own_slot, 1], ALONG, inner)
+    drain(window.at[own_slot, 1, pl.ds(sixth, 5 * sixth)], ALONG, outer)
     drain(halves.at[0], HALF)
     drain(partial.at[0], QUARTER)
     drain(fields.at[0], FIELD)
@@ -563,10 +582,10 @@
     ours = [handed(step, core) for step in steps] + [crossed(step) for step in steps]
     for_count(ours, lambda block: drain(block, COEFF_PARTNER))
     for_count([crossing(step) for step in steps], lambda block: drain(block, COEFF_BESIDE))
-    up = [above] + [jnp.logical_and(exists(-hop), above) for hop in range(1, levels)]
-    down = [below] + [jnp.logical_and(exists(hop), below) for hop in range(1, levels)]
-    for_count(up, lambda block: drain(block, COEFF_ABOVE))
-    for_count(down, lambda block: drain(block, COEFF_BELOW))
+    up_count = [above] + [jnp.logical_and(exists(-hop), above) for hop in range(1, levels)]
+    down_count = [below] + [jnp.logical_and(exists(hop), below) for hop in range(1, levels)]
+    for_count(up_count, lambda block: drain(block, COEFF_ABOVE))
+    for_count(down_count, lambda block: drain(block, COEFF_BELOW))
 
 
 def finish_kernel(count_ref, acc_ref, out_ref, staged, sem):

time: 44.2 us -> 42.8 us (0.968)
  Pallas kernels: 43.4 us -> 42 us
    pallas_call x1, Pallas kernels: 42.2 us -> 40.8 us  [body(): pl.pallas_call(functools.partial(exchange_kernel, levels, clusters), out_...]
where the time goes in v5:
time: 42.8 us; the launch traced here: 42.6 us
  Pallas kernels  42 us (98%)
  between operations  0.66 us (2%)
    pallas_call x1, Pallas kernels, body(): pl.pallas_call(functools.partial(exchange_kernel, levels, clusters), out_...  40.8 us
    pallas_call x1, Pallas kernels, body(): pl.pallas_call(finish_kernel, out_shape=jax.ShapeDtypeStruct((rows, vecs)...  1.21 us

profile of v5, /device:TPU:5, one launch (start us, length us, event | category | flops | bytes accessed | tf_op | source)
XLA Modules:
  0.0 42.6 jit_solution(2126064390195389339)
XLA Ops:
  0.7 40.8 %shard_map.91.acc_ref = f32[2,768,256]{2,1,0:T(8,128)S(1)} custom-call(s32[1,1]{1,0:T(1,128)S(6)} %copy.10.count_ref, s32[1,1,8]{2,1,0:T(1,128)} %near_source.1, s32[1,1,7]{2,1,0:T(1,128)} %far_source.1, bf16[1,1,768,512]{3,2,1,0:T(8,128)(2,1)} %vectors_ref.1, bf16[1,1,8,768,768]{4,3,2,1,0:T(8,128)(2,1)} %tiles_ref.1, bf16[1,1,768,128]{3,2,1,0:T(8,128)(2,1)} %basis_ref.1, ...), custom_call_target="tpu_custom_call" | custom-call | tf_op jit(solution)/shard_map/pallas_call | solution.py:629
  41.4 1.2 %shard_map.92 = f32[768,512]{1,0:T(8,128)} custom-call(s32[1,1]{1,0:T(1,128)S(6)} %copy.10.count_ref, f32[2,768,256]{2,1,0:T(8,128)S(1)} %shard_map.91.acc_ref), custom_call_target="tpu_custom_call" | custom-call | tf_op jit(solution)/shard_map/pallas_call | solution.py:682

commit v6 on v5

--- a/solution.py
+++ b/solution.py
@@ -10,7 +10,8 @@
 REACH = 4
 SLOTS = 2 * REACH + 2
 PIECES = 3
-SPANS = ((0, 1), (1, 3), (3, 5), (5, 6))
+UNITS = 12
+SPANS = ((8, 9), (0, 4), (4, 8), (9, 12))
 BESIDE, BELOW, ABOVE, PARTNER, FAR_BESIDE, BRIDGED = 0, 2, 4, 6, 8, 10
 DIAGONAL, FAR_DIAGONAL, SPAN = 12, 12 + PIECES, 12 + 2 * PIECES
 FAR_SPAN = SPAN + len(SPANS)
@@ -33,10 +34,11 @@
     HALF,
     QUARTER,
     LINE,
+    TOTAL,
     FIELD,
     FIELD_PAIR,
     PARENT,
-) = range(20)
+) = range(21)
 
 
 def contract(left, right):
@@ -76,8 +78,11 @@
     quarter_in,
     line_out,
     line_in,
+    total_out,
+    total_in,
     parents,
     fields,
+    field_ref,
     load_sem,
     send_sem,
     block_sem,
@@ -102,7 +107,7 @@
     rows, half = raw.shape[1:]
     vecs = 2 * half
     quarter = half // 2
-    sixth = rows // 6
+    unit = rows // UNITS
     piece = rows // PIECES
     tile_count = tiles.shape[0]
 
@@ -204,7 +209,7 @@
 
     def span_of(index):
         start, stop = SPANS[index]
-        return pl.ds(start * sixth, (stop - start) * sixth)
+        return pl.ds(start * unit, (stop - start) * unit)
 
     def send_rows(slot, part, span, target, arrival, peer, done, condition=None):
         send(
@@ -280,7 +285,10 @@
             wait_coeff(beside + 4 * step, crossed(step))
             hand_coeff(beside + 4 * step, crossed(step))
 
-    def near(slot, part, condition=None, first=False, spans=None):
+    def far_product(part):
+        return dot(basis[...], field_ref[:, part * half : (part + 1) * half])
+
+    def near(slot, part, condition=None, first=False, span=None, far=False):
         offset = slot - REACH - core
         place, hit = 0, 0
         for k in range(tile_count):
@@ -290,14 +298,13 @@
         scale = hit.astype(jnp.float32)
 
         def run():
-            if spans is None:
+            if span is None:
                 product = dot(tiles[place], window[slot, part]) * scale
             else:
-                product = 0.0
-                for start, stop in spans:
-                    span = slice(start * sixth, stop * sixth)
-                    product = product + dot(tiles[place, :, span], window[slot, part, span, :])
-                product = product * scale
+                lines = slice(span[0] * unit, span[1] * unit)
+                product = dot(tiles[place, :, lines], window[slot, part, lines, :]) * scale
+            if far:
+                product = product + far_product(part)
             if first:
                 acc[part] = product
             else:
@@ -368,20 +375,31 @@
     partial[column] += quarter_in[...]
 
     def line(turn):
-        for way, at, step in ((0, turn - 1, 4), (1, levels - turn, -4)):
-            here = level == at
-            if turn > 1:
-                receive(line_in.at[way], line_sem.at[way], here)
-            if turn < levels:
-
-                @pl.when(here)
+        ways = ((0, turn - 1, 4), (1, levels - turn, -4))
+        whole = 2 < levels == turn + 1
+        if turn > 1:
+            for way, at, _ in ways:
+                block = total_in if 2 < levels == turn else line_in.at[way]
+                receive(block, line_sem.at[way], level == at)
+        if turn < levels:
+            for way, at, step in ways:
+
+                @pl.when(level == at)
                 def _(way=way):
                     value = partial[column]
                     if turn > 1:
                         value = value + line_in[way]
-                    line_out[way] = value
-
-                send(line_out.at[way], line_in.at[way], line_sem.at[way], {"leaf": me + step}, LINE, here)
+                    if whole:
+                        value = value + line_in[1 - way]
+                        total_out[way] = value.astype(jnp.bfloat16)
+                    else:
+                        line_out[way] = value
+
+                peer = {"leaf": me + step}
+                if whole:
+                    send(total_out.at[way], total_in, line_sem.at[way], peer, TOTAL, level == at)
+                else:
+                    send(line_out.at[way], line_in.at[way], line_sem.at[way], peer, LINE, level == at)
 
     line(1)
     send_own(1, 0)
@@ -433,12 +451,15 @@
     wait_block(beside_slot, 1, BESIDE)
     inner_up = jnp.logical_and(relay_up, level < levels - 2)
     inner_down = jnp.logical_and(relay_down, level > 1)
+
+    def send_span(slot, index, target, peer, done, condition):
+        span = span_of(index)
+        send_rows(slot, 1, span, target, SPAN + index, peer, done, condition)
+
     for index in range(len(SPANS)):
-        span = span_of(index)
-        arrival = SPAN + index
-        up, down = (relay_up, relay_down) if index else (inner_up, inner_down)
-        send_rows(beside_slot, 1, span, core + 2, arrival, to_above, ALONG, up)
-        send_rows(beside_slot, 1, span, core + 6, arrival, to_below, ALONG, down)
+        up, down = (inner_up, inner_down) if index == 0 else (relay_up, relay_down)
+        send_span(beside_slot, index, core + 2, to_above, ALONG, up)
+        send_span(beside_slot, index, core + 6, to_below, ALONG, down)
     send_block(beside_slot, 1, beside_slot, FAR_BESIDE, to_partner, HAND_BESIDE)
     near(beside_slot, 1)
     for hop in range(3, levels):
@@ -449,7 +470,10 @@
     whole = partial[column]
     for way, condition in ((0, below), (1, above)):
         whole = whole + jnp.where(condition, line_in[way], 0.0)
-    parents[cluster] = whole.astype(jnp.bfloat16)
+    whole = whole.astype(jnp.bfloat16)
+    if levels > 2:
+        whole = jnp.where(jnp.logical_xor(above, below), total_in[...], whole)
+    parents[cluster] = whole
     for step in range(1, clusters):
         send(
             parents.at[cluster],
@@ -476,11 +500,10 @@
         hand_crossed(2)
     wait_block(below_slot, 1, BELOW, below)
     wait_block(above_slot, 1, ABOVE, above)
-    span = span_of(0)
     last_down = jnp.logical_and(relay_down, level == levels - 1)
     last_up = jnp.logical_and(relay_up, level == 0)
-    send_rows(below_slot, 1, span, core + 2, SPAN, to_beside, OVER_SPAN, last_down)
-    send_rows(above_slot, 1, span, core + 6, SPAN, to_beside, OVER_SPAN, last_up)
+    send_span(below_slot, 0, core + 2, to_beside, OVER_SPAN, last_down)
+    send_span(above_slot, 0, core + 6, to_beside, OVER_SPAN, last_up)
     hand_neighbours(1)
     near(below_slot, 1, below)
     near(above_slot, 1, above)
@@ -491,37 +514,44 @@
         wait_rows(diagonal_slot, 0, span, DIAGONAL + index, diagonal)
         send_rows(diagonal_slot, 0, span, diagonal_slot, arrival, to_partner, HAND_DIAGONAL, diagonal)
 
-    def own_first(index):
-        near(diagonal_slot, 0, diagonal, spans=((2 * index, 2 * index + 2),))
+    def own_first(index, far=False):
+        near(diagonal_slot, 0, diagonal, span=third(index), far=far)
 
     def far_first(index):
         wait_rows(far_diagonal_slot, 0, rows_of(index), FAR_DIAGONAL + index, diagonal)
-        near(far_diagonal_slot, 0, diagonal, spans=((2 * index, 2 * index + 2),))
+        near(far_diagonal_slot, 0, diagonal, span=third(index))
+
+    def third(index):
+        return (index * UNITS // PIECES, (index + 1) * UNITS // PIECES)
+
+    def wait_span(slot, index, arrival):
+        wait_rows(slot, 1, span_of(index), arrival + index, diagonal)
 
     def hand_second(index):
         span = span_of(index)
         arrival = FAR_SPAN + index
-        wait_rows(diagonal_slot, 1, span, SPAN + index, diagonal)
+        wait_span(diagonal_slot, index, SPAN)
         send_rows(diagonal_slot, 1, span, diagonal_slot, arrival, to_partner, HAND_DIAGONAL, diagonal)
 
-    def own_second(*indices):
-        near(diagonal_slot, 1, diagonal, spans=[SPANS[index] for index in indices])
-
-    def far_second(*indices):
-        for index in indices:
-            wait_rows(far_diagonal_slot, 1, span_of(index), FAR_SPAN + index, diagonal)
-        near(far_diagonal_slot, 1, diagonal, spans=[SPANS[index] for index in indices])
+    middle, later, ends = (0, 4), (4, 8), (8, 12)
+
+    def own_second(span, far=False):
+        near(diagonal_slot, 1, diagonal, span=span, far=far)
+
+    def far_second(span):
+        near(far_diagonal_slot, 1, diagonal, span=span)
 
     hand_first(0)
     own_first(0)
     wait_block(bridged_slot, 1, BRIDGED, bridged)
     near(bridged_slot, 1, bridged)
     hand_second(1)
-    own_second(1)
+    own_second(middle)
     hand_first(1)
     own_first(1)
     far_first(0)
-    far_second(1)
+    wait_span(far_diagonal_slot, 1, FAR_SPAN)
+    far_second(middle)
     next_place = 2 * core + 1 - column
     receive(fields.at[next_place], field_sem.at[0])
     pair = fields.at[pl.ds(2 * core, 2)]
@@ -530,7 +560,7 @@
         hand_crossed(hop)
     far_first(1)
     hand_second(2)
-    own_second(2)
+    own_second(later)
 
     steps = [step for hop in range(1, levels) for step in (-hop, hop)]
     theirs_count = [handed(step, other) for step in steps] + [crossed(step) for step in steps]
@@ -541,18 +571,25 @@
     field = dot(nested[...], jnp.concatenate([fields[k] for k in range(4)], axis=1))
     for m in range(coupling.shape[0]):
         field = field + dot(coupling[m], coeffs[far_ref[0, 0, m]])
-    field = field.astype(jnp.bfloat16)
-    for part in range(2):
-        acc[part] += dot(basis[...], field[:, part * half : (part + 1) * half])
+    field_ref[...] = field.astype(jnp.bfloat16)
+
+    @pl.when(jnp.logical_not(diagonal))
+    def _():
+        for part in range(2):
+            acc[part] += far_product(part)
+
 
     hand_first(2)
-    own_first(2)
+    own_first(2, far=True)
     hand_second(3)
-    far_second(2)
+    wait_span(far_diagonal_slot, 2, FAR_SPAN)
+    far_second(later)
     hand_second(0)
-    own_second(3, 0)
+    own_second(ends, far=True)
     far_first(2)
-    far_second(3, 0)
+    wait_span(far_diagonal_slot, 3, FAR_SPAN)
+    wait_span(far_diagonal_slot, 0, FAR_SPAN)
+    far_second(ends)
 
     whole_block = window.at[own_slot]
     for done, condition in (
@@ -562,23 +599,35 @@
         (TO_PARTNER, None),
         (HAND_BESIDE, None),
         (HAND_COLUMN, jnp.logical_or(hand_below, hand_above)),
-        (HAND_DIAGONAL, diagonal),
     ):
         drain(whole_block, done, condition)
     drain(window.at[own_slot, 0], OVER, relay_over)
-    drain(window.at[own_slot, 1, span_of(0)], OVER_SPAN, jnp.logical_or(last_down, last_up))
+
+    def drain_units(units, done, condition):
+        drain(window.at[own_slot, 1, pl.ds(0, units * unit)], done, condition)
+
     inner = jnp.logical_or(inner_up, inner_down)
     outer = jnp.logical_and(relay_over, jnp.logical_not(inner))
-    drain(window.at[own_slot, 1], ALONG, inner)
-    drain(window.at[own_slot, 1, pl.ds(sixth, 5 * sixth)], ALONG, outer)
+    last = jnp.logical_or(last_down, last_up)
+    drain_units(1, OVER_SPAN, last)
+    drain_units(UNITS, ALONG, inner)
+    drain_units(UNITS - 1, ALONG, outer)
+    drain(whole_block, HAND_DIAGONAL, diagonal)
     drain(halves.at[0], HALF)
     drain(partial.at[0], QUARTER)
     drain(fields.at[0], FIELD)
     drain(fields.at[pl.ds(0, 2)], FIELD_PAIR)
     for step in range(1, clusters):
         drain(parents.at[0], PARENT + step - 1)
-    drain(line_out.at[0], LINE, jnp.logical_xor(above, below))
-    drain(line_out, LINE, jnp.logical_and(above, below))
+    totals = [level == 1, level == levels - 2] if levels > 2 else [below & False] * 2
+    lines = [
+        jnp.logical_and(neighbour, jnp.logical_not(total))
+        for neighbour, total in zip((below, above), totals)
+    ]
+    drain_pair = ((line_out, LINE, lines), (total_out, TOTAL, totals))
+    for block, done, (one, two) in drain_pair:
+        drain(block.at[0], done, jnp.logical_xor(one, two))
+        drain(block, done, jnp.logical_and(one, two))
     ours = [handed(step, core) for step in steps] + [crossed(step) for step in steps]
     for_count(ours, lambda block: drain(block, COEFF_PARTNER))
     for_count([crossing(step) for step in steps], lambda block: drain(block, COEFF_BESIDE))
@@ -648,8 +697,11 @@
             pltpu.VMEM((rank, quarter), jnp.float32),
             pltpu.VMEM((2, rank, quarter), jnp.float32),
             pltpu.VMEM((2, rank, quarter), jnp.float32),
+            pltpu.VMEM((2, rank, quarter), jnp.bfloat16),
+            pltpu.VMEM((rank, quarter), jnp.bfloat16),
             pltpu.VMEM((clusters, rank, quarter), jnp.bfloat16),
             pltpu.VMEM((4, rank, quarter), jnp.bfloat16),
+            pltpu.VMEM((rank, vecs), jnp.bfloat16),
             dma((9,)),
             dma((PARENT + clusters - 1,)),
             dma((ARRIVALS,)),

time: 42.8 us -> 42.1 us (0.984)
  Pallas kernels: 42 us -> 41.3 us
    pallas_call x1, Pallas kernels: 40.8 us -> 40.1 us  [body(): pl.pallas_call(functools.partial(exchange_kernel, levels, clusters), out_...]
where the time goes in v6:
time: 42.1 us; the launch traced here: 41.9 us
  Pallas kernels  41.3 us (98%)
  between operations  0.66 us (2%)
    pallas_call x1, Pallas kernels, body(): pl.pallas_call(functools.partial(exchange_kernel, levels, clusters), out_...  40.1 us
    pallas_call x1, Pallas kernels, body(): pl.pallas_call(finish_kernel, out_shape=jax.ShapeDtypeStruct((rows, vecs)...  1.21 us

profile of v6, /device:TPU:5, one launch (start us, length us, event | category | flops | bytes accessed | tf_op | source)
XLA Modules:
  0.0 41.9 jit_solution(6795428085945489337)
XLA Ops:
  0.7 40.1 %shard_map.91.acc_ref = f32[2,768,256]{2,1,0:T(8,128)S(1)} custom-call(s32[1,1]{1,0:T(1,128)S(6)} %copy.10.count_ref, s32[1,1,8]{2,1,0:T(1,128)} %near_source.1, s32[1,1,7]{2,1,0:T(1,128)} %far_source.1, bf16[1,1,768,512]{3,2,1,0:T(8,128)(2,1)} %vectors_ref.1, bf16[1,1,8,768,768]{4,3,2,1,0:T(8,128)(2,1)} %tiles_ref.1, bf16[1,1,768,128]{3,2,1,0:T(8,128)(2,1)} %basis_ref.1, ...), custom_call_target="tpu_custom_call" | custom-call | tf_op jit(solution)/shard_map/pallas_call | solution.py:678
  40.7 1.2 %shard_map.92 = f32[768,512]{1,0:T(8,128)} custom-call(s32[1,1]{1,0:T(1,128)S(6)} %copy.10.count_ref, f32[2,768,256]{2,1,0:T(8,128)S(1)} %shard_map.91.acc_ref), custom_call_target="tpu_custom_call" | custom-call | tf_op jit(solution)/shard_map/pallas_call | solution.py:734

commit v7 on v6

--- a/solution.py
+++ b/solution.py
@@ -11,7 +11,7 @@
 SLOTS = 2 * REACH + 2
 PIECES = 3
 UNITS = 12
-SPANS = ((8, 9), (0, 4), (4, 8), (9, 12))
+SPANS = ((8, 9), (0, 4), (4, 8), (9, 11), (11, 12))
 BESIDE, BELOW, ABOVE, PARTNER, FAR_BESIDE, BRIDGED = 0, 2, 4, 6, 8, 10
 DIAGONAL, FAR_DIAGONAL, SPAN = 12, 12 + PIECES, 12 + 2 * PIECES
 FAR_SPAN = SPAN + len(SPANS)
@@ -585,10 +585,11 @@
     wait_span(far_diagonal_slot, 2, FAR_SPAN)
     far_second(later)
     hand_second(0)
+    hand_second(4)
     own_second(ends, far=True)
     far_first(2)
-    wait_span(far_diagonal_slot, 3, FAR_SPAN)
-    wait_span(far_diagonal_slot, 0, FAR_SPAN)
+    for index in (0, 3, 4):
+        wait_span(far_diagonal_slot, index, FAR_SPAN)
     far_second(ends)
 
     whole_block = window.at[own_slot]

time: 42.1 us -> 42.2 us (level)
  no operation moved by 1% of the time
where the time goes in v7:
time: 42.2 us; the launch traced here: 42 us
  Pallas kernels  41.4 us (98%)
  between operations  0.66 us (2%)
    pallas_call x1, Pallas kernels, body(): pl.pallas_call(functools.partial(exchange_kernel, levels, clusters), out_...  40.1 us
    pallas_call x1, Pallas kernels, body(): pl.pallas_call(finish_kernel, out_shape=jax.ShapeDtypeStruct((rows, vecs)...  1.21 us

profile of v7, /device:TPU:5, one launch (start us, length us, event | category | flops | bytes accessed | tf_op | source)
XLA Modules:
  0.0 42.0 jit_solution(15476285825981494740)
XLA Ops:
  0.7 40.1 %shard_map.91.acc_ref = f32[2,768,256]{2,1,0:T(8,128)S(1)} custom-call(s32[1,1]{1,0:T(1,128)S(6)} %copy.10.count_ref, s32[1,1,8]{2,1,0:T(1,128)} %near_source.1, s32[1,1,7]{2,1,0:T(1,128)} %far_source.1, bf16[1,1,768,512]{3,2,1,0:T(8,128)(2,1)} %vectors_ref.1, bf16[1,1,8,768,768]{4,3,2,1,0:T(8,128)(2,1)} %tiles_ref.1, bf16[1,1,768,128]{3,2,1,0:T(8,128)(2,1)} %basis_ref.1, ...), custom_call_target="tpu_custom_call" | custom-call | tf_op jit(solution)/shard_map/pallas_call | solution.py:679
  40.8 1.2 %shard_map.92 = f32[768,512]{1,0:T(8,128)} custom-call(s32[1,1]{1,0:T(1,128)S(6)} %copy.10.count_ref, f32[2,768,256]{2,1,0:T(8,128)S(1)} %shard_map.91.acc_ref), custom_call_target="tpu_custom_call" | custom-call | tf_op jit(solution)/shard_map/pallas_call | solution.py:735

commit v8 on v6

--- a/solution.py
+++ b/solution.py
@@ -582,9 +582,9 @@
     hand_first(2)
     own_first(2, far=True)
     hand_second(3)
+    hand_second(0)
     wait_span(far_diagonal_slot, 2, FAR_SPAN)
     far_second(later)
-    hand_second(0)
     own_second(ends, far=True)
     far_first(2)
     wait_span(far_diagonal_slot, 3, FAR_SPAN)

time: 42.1 us -> 41.9 us (level)
  no operation moved by 1% of the time
where the time goes in v8:
time: 41.9 us; the launch traced here: 41.8 us
  Pallas kernels  41.1 us (98%)
  between operations  0.66 us (2%)
    pallas_call x1, Pallas kernels, body(): pl.pallas_call(functools.partial(exchange_kernel, levels, clusters), out_...  39.9 us
    pallas_call x1, Pallas kernels, body(): pl.pallas_call(finish_kernel, out_shape=jax.ShapeDtypeStruct((rows, vecs)...  1.21 us

profile of v8, /device:TPU:5, one launch (start us, length us, event | category | flops | bytes accessed | tf_op | source)
XLA Modules:
  0.0 41.8 jit_solution(8415910370867349636)
XLA Ops:
  0.7 39.9 %shard_map.91.acc_ref = f32[2,768,256]{2,1,0:T(8,128)S(1)} custom-call(s32[1,1]{1,0:T(1,128)S(6)} %copy.10.count_ref, s32[1,1,8]{2,1,0:T(1,128)} %near_source.1, s32[1,1,7]{2,1,0:T(1,128)} %far_source.1, bf16[1,1,768,512]{3,2,1,0:T(8,128)(2,1)} %vectors_ref.1, bf16[1,1,8,768,768]{4,3,2,1,0:T(8,128)(2,1)} %tiles_ref.1, bf16[1,1,768,128]{3,2,1,0:T(8,128)(2,1)} %basis_ref.1, ...), custom_call_target="tpu_custom_call" | custom-call | tf_op jit(solution)/shard_map/pallas_call | solution.py:678
  40.6 1.2 %shard_map.92 = f32[768,512]{1,0:T(8,128)} custom-call(s32[1,1]{1,0:T(1,128)S(6)} %copy.10.count_ref, f32[2,768,256]{2,1,0:T(8,128)S(1)} %shard_map.91.acc_ref), custom_call_target="tpu_custom_call" | custom-call | tf_op jit(solution)/shard_map/pallas_call | solution.py:734
